TPU v7x, 32 devices: a whole 2x2x4 slice. The times are simulated.
32 devices in a mesh: gx: 4 (over x, core), gy: 8 (over z, y).
Axes of the slice: x: 2, y: 2, z: 4, core: 2. Of those that a mesh axis runs over, the one named last changes fastest.
Arguments:
- electric: float32 [3, 64, 128, 256], P(None, 'gx', 'gy'), may hold values from -6 to 6
- magnetic: float32 [3, 64, 128, 256], P(None, 'gx', 'gy'), may hold values from -6 to 6
- aux_electric: float32 [6, 64, 128, 256], P(None, 'gx', 'gy'), may hold values from -3 to 3
- aux_magnetic: float32 [6, 64, 128, 256], P(None, 'gx', 'gy'), may hold values from -3 to 3
- grades: int32 [3, 64, 128, 256], P(None, 'gx', 'gy'), may hold values from 0 to 3
- permittivity: float32 [64, 128, 256], P('gx', 'gy'), may hold values from 1 to 8
- dipole_cell: int32 [3, 16384], P(None, ('gx', 'gy')), may hold values from 0 to 255, as said below
- dipole_port: int32 [16384], P(('gx', 'gy')), may hold values from 0 to 511
- live_count: int32 [32], P(('gx', 'gy')), may hold values from 1 to 512, as said below
- injection: bfloat16 [16384, 512], P(('gx', 'gy')), may hold values from -0.25 to 0.25
- waveform: bfloat16 [512, 16], replicated, may hold values from -6 to 6
Outputs:
- electric_out: float32 [3, 64, 128, 256], P(None, 'gx', 'gy')
- magnetic_out: float32 [3, 64, 128, 256], P(None, 'gx', 'gy')
- port_power: float32 [16, 512], replicated
Inputs may be any that keep to these rules, and one draw needn't show every extreme that they name: `dipole_cell`: slot s lies in the block of cells held by the device that holds slot s. The live slots of a device are its first live_count ones; some device has all 512 live.
All inputs are finite; a program needn't handle non-finite values.
Results may differ from a plain program's by a relative error of at most 0.0003.
Values sent between devices are 32-bit elements; how exact they have to be, the bound alone decides.
No kernel may reach another device: no remote copies, remote signals or barrier semaphores. Data moves between devices by JAX's collectives and lax.ppermute only.
A program may use at most 128 MiB of HBM per device.

v0:
```python
import jax
import jax.numpy as jnp
from jax import lax
from jax.sharding import PartitionSpec as P

courant = 0.55
absorb_keep = (0.0, 0.92, 0.75, 0.45)
absorb_take = (0.0, -0.06, -0.18, -0.35)
derivative_pairs = ((2, 1), (1, 2), (0, 2), (2, 0), (1, 0), (0, 1))


def passed_along(block, axis, distance):
    devices = range(lax.axis_size(axis))
    route = [(i - distance, i) for i in devices if i - distance in devices]
    return lax.ppermute(block, axis, route)


def difference(values, axis, plane, forward):
    length = values.shape[axis]
    if plane is None:
        shape = list(values.shape)
        shape[axis] = 1
        plane = jnp.zeros(shape, values.dtype)
    if forward:
        after = jnp.concatenate([lax.slice_in_dim(values, 1, length, axis=axis), plane], axis)
        return after - values
    before = jnp.concatenate([plane, lax.slice_in_dim(values, 0, length - 1, axis=axis)], axis)
    return values - before


def grade_table(grades, table):
    result = jnp.zeros(grades.shape, jnp.float32)
    for level in range(1, 4):
        result = result + jnp.where(grades == level, table[level], 0.0)
    return result


def curl_parts(field, auxiliary, keep, take, planes, forward):
    terms = []
    updated = []
    for number, (component, axis) in enumerate(derivative_pairs):
        plane = None
        if planes is not None and axis == 0:
            plane = planes[0][component - 1]
        if planes is not None and axis == 1:
            plane = planes[1][component // 2]
        slope = difference(field[component], axis, plane, forward)
        carried = keep[axis] * auxiliary[number] + take[axis] * slope
        terms.append(slope + carried)
        updated.append(carried)
    rotation = (terms[0] - terms[1], terms[2] - terms[3], terms[4] - terms[5])
    return (rotation, tuple(updated))


def inject(z_plane, current_now, cell_table, depth_table):
    weighted = cell_table * current_now[:, None]
    source = lax.dot_general(
        weighted, depth_table, (((0,), (0,)), ((), ())), precision=lax.Precision.HIGHEST
    )
    return z_plane - courant * source.reshape(z_plane.shape)


def read_cells(z_plane, cell_table, depth_table):
    rows = z_plane.reshape(cell_table.shape[1], depth_table.shape[1])
    picked = jnp.dot(cell_table, rows, precision=lax.Precision.HIGHEST)
    return jnp.sum(picked * depth_table, axis=1)


def note_power(record, drive, index):
    return lax.dynamic_update_slice_in_dim(record, drive[None, :], index, 0)


def local(
    electric,
    magnetic,
    aux_electric,
    aux_magnetic,
    grades,
    permittivity,
    dipole_cell,
    dipole_port,
    live_count,
    injection,
    waveform,
):
    depth_x, depth_y, depth_z = electric.shape[1:]
    slots = dipole_cell.shape[1]
    ports, steps = waveform.shape
    row_index = lax.axis_index("gx")
    col_index = lax.axis_index("gy")
    plane_cell = (dipole_cell[0] - row_index * depth_x) * depth_y + (
        dipole_cell[1] - col_index * depth_y
    )
    cell_table = (
        plane_cell[:, None] == jnp.arange(depth_x * depth_y, dtype=jnp.int32)[None, :]
    ).astype(jnp.float32)
    depth_table = (dipole_cell[2][:, None] == jnp.arange(depth_z, dtype=jnp.int32)[None, :]).astype(
        jnp.float32
    )
    live = (jnp.arange(slots, dtype=jnp.int32) < live_count[0]).astype(jnp.float32)
    current = jnp.dot(injection, waveform, preferred_element_type=jnp.float32) * live[:, None]
    members = (dipole_port[:, None] == jnp.arange(ports, dtype=jnp.int32)[None, :]).astype(
        jnp.float32
    )
    factor = courant / permittivity
    keep = grade_table(grades, absorb_keep)
    take = grade_table(grades, absorb_take)
    record = jnp.zeros((steps, slots), jnp.float32)

    def turn_parts(step, carry):
        field_e, field_h, memory_e, memory_h, record = carry
        next_x = passed_along(jnp.stack([field_e[1][0:1], field_e[2][0:1]]), "gx", -1)
        next_y = passed_along(jnp.stack([field_e[0][:, 0:1], field_e[2][:, 0:1]]), "gy", -1)
        rotation, memory_e = curl_parts(field_e, memory_e, keep, take, (next_x, next_y), True)
        field_h = tuple((field_h[number] - courant * rotation[number] for number in range(3)))
        prior_x = passed_along(jnp.stack([field_h[1][-1:], field_h[2][-1:]]), "gx", 1)
        prior_y = passed_along(jnp.stack([field_h[0][:, -1:], field_h[2][:, -1:]]), "gy", 1)
        rotation, memory_h = curl_parts(field_h, memory_h, keep, take, (prior_x, prior_y), False)
        current_now = lax.dynamic_slice_in_dim(current, step, 1, 1)[:, 0]
        z_plane = inject(field_e[2] + factor * rotation[2], current_now, cell_table, depth_table)
        field_e = (field_e[0] + factor * rotation[0], field_e[1] + factor * rotation[1], z_plane)
        drive = current_now * read_cells(z_plane, cell_table, depth_table)
        record = note_power(record, drive, step)
        return (field_e, field_h, memory_e, memory_h, record)

    start_state = (
        tuple((electric[number] for number in range(3))),
        tuple((magnetic[number] for number in range(3))),
        tuple((aux_electric[number] for number in range(6))),
        tuple((aux_magnetic[number] for number in range(6))),
        record,
    )
    parts_e, parts_h, parts_me, parts_mh, record = lax.fori_loop(0, steps, turn_parts, start_state)
    electric = jnp.stack(parts_e)
    magnetic = jnp.stack(parts_h)
    partial_value = jnp.dot(record, members, precision=lax.Precision.HIGHEST)
    port_power = lax.psum(partial_value, ("gx", "gy"))
    return (electric, magnetic, port_power)


def solution(mesh):
    in_specs = (
        P(None, "gx", "gy", None),
        P(None, "gx", "gy", None),
        P(None, "gx", "gy", None),
        P(None, "gx", "gy", None),
        P(None, "gx", "gy", None),
        P("gx", "gy", None),
        P(None, ("gx", "gy")),
        P(("gx", "gy")),
        P(("gx", "gy")),
        P(("gx", "gy"), None),
        P(),
    )
    out_specs = (P(None, "gx", "gy", None), P(None, "gx", "gy", None), P())
    return jax.shard_map(local, mesh=mesh, in_specs=in_specs, out_specs=out_specs, check_vma=False)
```

profile of v0, /device:TPU:0, one launch (start us, length us, event | category | flops | bytes accessed | tf_op | source)
XLA Modules:
  0.0 605.0 jit_solution(2541762445763992828)
XLA Ops:
  10.5 545.4 %while.50 = (s32[]{:T(128)}, f32[16,16,256]{2,1,0:T(8,128)S(1)}, f32[16,16,256]{2,1,0:T(8,128)S(1)}, f32[16,16,256]{2,1,0:T(8,128)S(1)}, f32[16,16,256]{2,1,0:T(...) while((s32[]{:T(128)}, f32[16,16,256]{2,1,0:T(8,128)S(1)}, ...), condition=%wide.region_2.3_spmd.clone, body=%wide.region_0.2_spmd.clone.sunk | while | flops 812285952 | bytes 56044672 | solution.py:133
  20.5 2.4 multiply_subtract_fusion.7
  23.5 5.5 collective-permute-start.2
  30.9 2.8 collective-permute-start.3
  39.1 2.4 multiply_add_fusion.5
  52.6 2.4 multiply_subtract_fusion.7
  55.6 5.4 collective-permute-start.2
  63.0 3.8 collective-permute-start.3
  72.2 2.4 multiply_add_fusion.5
  85.7 2.4 multiply_subtract_fusion.7
  88.7 5.2 collective-permute-start.2
  95.8 5.3 collective-permute-start.3
  106.5 2.4 multiply_add_fusion.5
  120.0 2.4 multiply_subtract_fusion.7
  123.0 5.2 collective-permute-start.2
  130.1 5.3 collective-permute-start.3
  140.8 2.4 multiply_add_fusion.5
  154.3 2.4 multiply_subtract_fusion.7
  157.3 5.2 collective-permute-start.2
  164.4 5.3 collective-permute-start.3
  175.1 2.4 multiply_add_fusion.5
  188.6 2.4 multiply_subtract_fusion.7
  191.6 5.2 collective-permute-start.2
  198.7 5.3 collective-permute-start.3
  209.4 2.4 multiply_add_fusion.5
  222.9 2.4 multiply_subtract_fusion.7
  225.9 5.2 collective-permute-start.2
  233.0 5.3 collective-permute-start.3
  243.7 2.4 multiply_add_fusion.5
  257.2 2.4 multiply_subtract_fusion.7
  260.2 5.2 collective-permute-start.2
  267.3 5.3 collective-permute-start.3
  278.0 2.4 multiply_add_fusion.5
  291.5 2.4 multiply_subtract_fusion.7
  294.5 5.2 collective-permute-start.2
  301.6 5.3 collective-permute-start.3
  312.3 2.4 multiply_add_fusion.5
  325.8 2.4 multiply_subtract_fusion.7
  328.8 5.2 collective-permute-start.2
  335.9 5.3 collective-permute-start.3
  346.6 2.4 multiply_add_fusion.5
  360.1 2.4 multiply_subtract_fusion.7
  363.1 5.2 collective-permute-start.2
  370.2 5.3 collective-permute-start.3
  380.9 2.4 multiply_add_fusion.5
  394.4 2.4 multiply_subtract_fusion.7
  397.4 5.2 collective-permute-start.2
  404.5 5.3 collective-permute-start.3
  415.2 2.4 multiply_add_fusion.5
  428.7 2.4 multiply_subtract_fusion.7
  431.7 5.2 collective-permute-start.2
  438.8 5.3 collective-permute-start.3
  449.4 2.4 multiply_add_fusion.5
  463.0 2.4 multiply_subtract_fusion.7
  466.0 5.2 collective-permute-start.2
  473.1 5.3 collective-permute-start.3
  497.3 2.4 multiply_subtract_fusion.7
  500.3 5.2 collective-permute-start.2
  507.4 5.3 collective-permute-start.3
  531.6 2.4 multiply_subtract_fusion.7
  534.6 5.2 collective-permute-start.2
  541.7 5.3 collective-permute-start.3
  552.3 2.4 multiply_add_fusion.5
  557.2 45.9 %psum.7 = f32[16,512]{1,0:T(8,128)} all-reduce(f32[16,512]{1,0:T(8,128)S(1)} %fusion.27), channel_id=1, replica_groups=mesh['gx'=4,'gy'=8] {'gx','gy'}, use_global_device_ids=true, to_apply=%region_3.4 | all-reduce | flops 8192 | bytes 65536 | tf_op jit(solution)/shard_map/psum | solution.py:137
  (1454 shorter events, 313.3 us)
Async XLA Ops:
  10.6 9.9 %collective-permute-start.1 = (f32[2,16,1,256]{3,2,1,0:T(1,128)S(1)}, f32[2,16,1,256]{3,2,1,0:T(1,128)S(1)}, u32[]{:S(2)}, u32[]{:S(2)}) collective-permute-start(f32[2,16,1,256]{3,2,1,0:T(1,128)S(1)} %pad_maximum_fusion.11), channel_id=1, source_target_pairs={{1,0},{2,1},{3,2},{4,3},{5,4},{6,5},{7,6},{9,8},{10,9},{11,10},{12... | collective-permute-start | bytes 98312 | tf_op jit(solution)/shard_map/while/body/eval_jaxpr/ppermute | solution.py:15
  11.9 8.5 %collective-permute-start = (f32[2,1,16,256]{3,2,1,0:T(8,128)S(1)}, f32[2,1,16,256]{3,2,1,0:T(8,128)S(1)}, u32[]{:S(2)}, u32[]{:S(2)}) collective-permute-start(f32[2,1,16,256]{3,2,1,0:T(8,128)S(1)} %pad_maximum_fusion.10), channel_id=1, source_target_pairs={{8,0},{16,8},{24,16},{9,1},{17,9},{25,17},{10,2},{18,10},{26,18},{... | collective-permute-start | bytes 98312 | tf_op jit(solution)/shard_map/while/body/eval_jaxpr/ppermute | solution.py:15
  23.5 10.2 %collective-permute-start.2 = (f32[2,16,1,256]{3,2,1,0:T(1,128)S(1)}, f32[2,16,1,256]{3,2,1,0:T(1,128)S(1)}, u32[]{:S(2)}, u32[]{:S(2)}) collective-permute-start(f32[2,16,1,256]{3,2,1,0:T(1,128)S(1)} %pad_maximum_fusion.12), channel_id=1, source_target_pairs={{0,1},{1,2},{2,3},{3,4},{4,5},{5,6},{6,7},{8,9},{9,10},{10,11},{11... | collective-permute-start | bytes 98312 | tf_op jit(solution)/shard_map/while/body/eval_jaxpr/ppermute | solution.py:15
  30.9 3.6 collective-permute-start.3
  42.7 9.9 %collective-permute-start.1 = (f32[2,16,1,256]{3,2,1,0:T(1,128)S(1)}, f32[2,16,1,256]{3,2,1,0:T(1,128)S(1)}, u32[]{:S(2)}, u32[]{:S(2)}) collective-permute-start(f32[2,16,1,256]{3,2,1,0:T(1,128)S(1)} %pad_maximum_fusion.11), channel_id=1, source_target_pairs={{1,0},{2,1},{3,2},{4,3},{5,4},{6,5},{7,6},{9,8},{10,9},{11,10},{12... | collective-permute-start | bytes 98312 | tf_op jit(solution)/shard_map/while/body/eval_jaxpr/ppermute | solution.py:15
  44.0 8.5 %collective-permute-start = (f32[2,1,16,256]{3,2,1,0:T(8,128)S(1)}, f32[2,1,16,256]{3,2,1,0:T(8,128)S(1)}, u32[]{:S(2)}, u32[]{:S(2)}) collective-permute-start(f32[2,1,16,256]{3,2,1,0:T(8,128)S(1)} %pad_maximum_fusion.10), channel_id=1, source_target_pairs={{8,0},{16,8},{24,16},{9,1},{17,9},{25,17},{10,2},{18,10},{26,18},{... | collective-permute-start | bytes 98312 | tf_op jit(solution)/shard_map/while/body/eval_jaxpr/ppermute | solution.py:15
  55.6 11.2 %collective-permute-start.2 = (f32[2,16,1,256]{3,2,1,0:T(1,128)S(1)}, f32[2,16,1,256]{3,2,1,0:T(1,128)S(1)}, u32[]{:S(2)}, u32[]{:S(2)}) collective-permute-start(f32[2,16,1,256]{3,2,1,0:T(1,128)S(1)} %pad_maximum_fusion.12), channel_id=1, source_target_pairs={{0,1},{1,2},{2,3},{3,4},{4,5},{5,6},{6,7},{8,9},{9,10},{10,11},{11... | collective-permute-start | bytes 98312 | tf_op jit(solution)/shard_map/while/body/eval_jaxpr/ppermute | solution.py:15
  63.0 4.7 collective-permute-start.3
  75.8 9.9 %collective-permute-start.1 = (f32[2,16,1,256]{3,2,1,0:T(1,128)S(1)}, f32[2,16,1,256]{3,2,1,0:T(1,128)S(1)}, u32[]{:S(2)}, u32[]{:S(2)}) collective-permute-start(f32[2,16,1,256]{3,2,1,0:T(1,128)S(1)} %pad_maximum_fusion.11), channel_id=1, source_target_pairs={{1,0},{2,1},{3,2},{4,3},{5,4},{6,5},{7,6},{9,8},{10,9},{11,10},{12... | collective-permute-start | bytes 98312 | tf_op jit(solution)/shard_map/while/body/eval_jaxpr/ppermute | solution.py:15
  77.1 8.5 %collective-permute-start = (f32[2,1,16,256]{3,2,1,0:T(8,128)S(1)}, f32[2,1,16,256]{3,2,1,0:T(8,128)S(1)}, u32[]{:S(2)}, u32[]{:S(2)}) collective-permute-start(f32[2,1,16,256]{3,2,1,0:T(8,128)S(1)} %pad_maximum_fusion.10), channel_id=1, source_target_pairs={{8,0},{16,8},{24,16},{9,1},{17,9},{25,17},{10,2},{18,10},{26,18},{... | collective-permute-start | bytes 98312 | tf_op jit(solution)/shard_map/while/body/eval_jaxpr/ppermute | solution.py:15
  88.7 12.4 %collective-permute-start.2 = (f32[2,16,1,256]{3,2,1,0:T(1,128)S(1)}, f32[2,16,1,256]{3,2,1,0:T(1,128)S(1)}, u32[]{:S(2)}, u32[]{:S(2)}) collective-permute-start(f32[2,16,1,256]{3,2,1,0:T(1,128)S(1)} %pad_maximum_fusion.12), channel_id=1, source_target_pairs={{0,1},{1,2},{2,3},{3,4},{4,5},{5,6},{6,7},{8,9},{9,10},{10,11},{11... | collective-permute-start | bytes 98312 | tf_op jit(solution)/shard_map/while/body/eval_jaxpr/ppermute | solution.py:15
  95.8 6.1 %collective-permute-start.3 = (f32[2,1,16,256]{3,2,1,0:T(8,128)S(1)}, f32[2,1,16,256]{3,2,1,0:T(8,128)S(1)}, u32[]{:S(2)}, u32[]{:S(2)}) collective-permute-start(f32[2,1,16,256]{3,2,1,0:T(8,128)S(1)} %pad_maximum_fusion.13), channel_id=1, source_target_pairs={{0,8},{8,16},{16,24},{1,9},{9,17},{17,25},{2,10},{10,18},{18,26},{... | collective-permute-start | bytes 98312 | tf_op jit(solution)/shard_map/while/body/eval_jaxpr/ppermute | solution.py:15
  110.1 9.9 %collective-permute-start.1 = (f32[2,16,1,256]{3,2,1,0:T(1,128)S(1)}, f32[2,16,1,256]{3,2,1,0:T(1,128)S(1)}, u32[]{:S(2)}, u32[]{:S(2)}) collective-permute-start(f32[2,16,1,256]{3,2,1,0:T(1,128)S(1)} %pad_maximum_fusion.11), channel_id=1, source_target_pairs={{1,0},{2,1},{3,2},{4,3},{5,4},{6,5},{7,6},{9,8},{10,9},{11,10},{12... | collective-permute-start | bytes 98312 | tf_op jit(solution)/shard_map/while/body/eval_jaxpr/ppermute | solution.py:15
  111.4 8.5 %collective-permute-start = (f32[2,1,16,256]{3,2,1,0:T(8,128)S(1)}, f32[2,1,16,256]{3,2,1,0:T(8,128)S(1)}, u32[]{:S(2)}, u32[]{:S(2)}) collective-permute-start(f32[2,1,16,256]{3,2,1,0:T(8,128)S(1)} %pad_maximum_fusion.10), channel_id=1, source_target_pairs={{8,0},{16,8},{24,16},{9,1},{17,9},{25,17},{10,2},{18,10},{26,18},{... | collective-permute-start | bytes 98312 | tf_op jit(solution)/shard_map/while/body/eval_jaxpr/ppermute | solution.py:15
  123.0 12.4 %collective-permute-start.2 = (f32[2,16,1,256]{3,2,1,0:T(1,128)S(1)}, f32[2,16,1,256]{3,2,1,0:T(1,128)S(1)}, u32[]{:S(2)}, u32[]{:S(2)}) collective-permute-start(f32[2,16,1,256]{3,2,1,0:T(1,128)S(1)} %pad_maximum_fusion.12), channel_id=1, source_target_pairs={{0,1},{1,2},{2,3},{3,4},{4,5},{5,6},{6,7},{8,9},{9,10},{10,11},{11... | collective-permute-start | bytes 98312 | tf_op jit(solution)/shard_map/while/body/eval_jaxpr/ppermute | solution.py:15
  130.1 6.1 %collective-permute-start.3 = (f32[2,1,16,256]{3,2,1,0:T(8,128)S(1)}, f32[2,1,16,256]{3,2,1,0:T(8,128)S(1)}, u32[]{:S(2)}, u32[]{:S(2)}) collective-permute-start(f32[2,1,16,256]{3,2,1,0:T(8,128)S(1)} %pad_maximum_fusion.13), channel_id=1, source_target_pairs={{0,8},{8,16},{16,24},{1,9},{9,17},{17,25},{2,10},{10,18},{18,26},{... | collective-permute-start | bytes 98312 | tf_op jit(solution)/shard_map/while/body/eval_jaxpr/ppermute | solution.py:15
  144.4 9.9 %collective-permute-start.1 = (f32[2,16,1,256]{3,2,1,0:T(1,128)S(1)}, f32[2,16,1,256]{3,2,1,0:T(1,128)S(1)}, u32[]{:S(2)}, u32[]{:S(2)}) collective-permute-start(f32[2,16,1,256]{3,2,1,0:T(1,128)S(1)} %pad_maximum_fusion.11), channel_id=1, source_target_pairs={{1,0},{2,1},{3,2},{4,3},{5,4},{6,5},{7,6},{9,8},{10,9},{11,10},{12... | collective-permute-start | bytes 98312 | tf_op jit(solution)/shard_map/while/body/eval_jaxpr/ppermute | solution.py:15
  145.7 8.5 %collective-permute-start = (f32[2,1,16,256]{3,2,1,0:T(8,128)S(1)}, f32[2,1,16,256]{3,2,1,0:T(8,128)S(1)}, u32[]{:S(2)}, u32[]{:S(2)}) collective-permute-start(f32[2,1,16,256]{3,2,1,0:T(8,128)S(1)} %pad_maximum_fusion.10), channel_id=1, source_target_pairs={{8,0},{16,8},{24,16},{9,1},{17,9},{25,17},{10,2},{18,10},{26,18},{... | collective-permute-start | bytes 98312 | tf_op jit(solution)/shard_map/while/body/eval_jaxpr/ppermute | solution.py:15
  157.3 12.4 %collective-permute-start.2 = (f32[2,16,1,256]{3,2,1,0:T(1,128)S(1)}, f32[2,16,1,256]{3,2,1,0:T(1,128)S(1)}, u32[]{:S(2)}, u32[]{:S(2)}) collective-permute-start(f32[2,16,1,256]{3,2,1,0:T(1,128)S(1)} %pad_maximum_fusion.12), channel_id=1, source_target_pairs={{0,1},{1,2},{2,3},{3,4},{4,5},{5,6},{6,7},{8,9},{9,10},{10,11},{11... | collective-permute-start | bytes 98312 | tf_op jit(solution)/shard_map/while/body/eval_jaxpr/ppermute | solution.py:15
  164.4 6.1 %collective-permute-start.3 = (f32[2,1,16,256]{3,2,1,0:T(8,128)S(1)}, f32[2,1,16,256]{3,2,1,0:T(8,128)S(1)}, u32[]{:S(2)}, u32[]{:S(2)}) collective-permute-start(f32[2,1,16,256]{3,2,1,0:T(8,128)S(1)} %pad_maximum_fusion.13), channel_id=1, source_target_pairs={{0,8},{8,16},{16,24},{1,9},{9,17},{17,25},{2,10},{10,18},{18,26},{... | collective-permute-start | bytes 98312 | tf_op jit(solution)/shard_map/while/body/eval_jaxpr/ppermute | solution.py:15
  178.7 9.9 %collective-permute-start.1 = (f32[2,16,1,256]{3,2,1,0:T(1,128)S(1)}, f32[2,16,1,256]{3,2,1,0:T(1,128)S(1)}, u32[]{:S(2)}, u32[]{:S(2)}) collective-permute-start(f32[2,16,1,256]{3,2,1,0:T(1,128)S(1)} %pad_maximum_fusion.11), channel_id=1, source_target_pairs={{1,0},{2,1},{3,2},{4,3},{5,4},{6,5},{7,6},{9,8},{10,9},{11,10},{12... | collective-permute-start | bytes 98312 | tf_op jit(solution)/shard_map/while/body/eval_jaxpr/ppermute | solution.py:15
  180.0 8.5 %collective-permute-start = (f32[2,1,16,256]{3,2,1,0:T(8,128)S(1)}, f32[2,1,16,256]{3,2,1,0:T(8,128)S(1)}, u32[]{:S(2)}, u32[]{:S(2)}) collective-permute-start(f32[2,1,16,256]{3,2,1,0:T(8,128)S(1)} %pad_maximum_fusion.10), channel_id=1, source_target_pairs={{8,0},{16,8},{24,16},{9,1},{17,9},{25,17},{10,2},{18,10},{26,18},{... | collective-permute-start | bytes 98312 | tf_op jit(solution)/shard_map/while/body/eval_jaxpr/ppermute | solution.py:15
  191.6 12.4 %collective-permute-start.2 = (f32[2,16,1,256]{3,2,1,0:T(1,128)S(1)}, f32[2,16,1,256]{3,2,1,0:T(1,128)S(1)}, u32[]{:S(2)}, u32[]{:S(2)}) collective-permute-start(f32[2,16,1,256]{3,2,1,0:T(1,128)S(1)} %pad_maximum_fusion.12), channel_id=1, source_target_pairs={{0,1},{1,2},{2,3},{3,4},{4,5},{5,6},{6,7},{8,9},{9,10},{10,11},{11... | collective-permute-start | bytes 98312 | tf_op jit(solution)/shard_map/while/body/eval_jaxpr/ppermute | solution.py:15
  198.7 6.1 %collective-permute-start.3 = (f32[2,1,16,256]{3,2,1,0:T(8,128)S(1)}, f32[2,1,16,256]{3,2,1,0:T(8,128)S(1)}, u32[]{:S(2)}, u32[]{:S(2)}) collective-permute-start(f32[2,1,16,256]{3,2,1,0:T(8,128)S(1)} %pad_maximum_fusion.13), channel_id=1, source_target_pairs={{0,8},{8,16},{16,24},{1,9},{9,17},{17,25},{2,10},{10,18},{18,26},{... | collective-permute-start | bytes 98312 | tf_op jit(solution)/shard_map/while/body/eval_jaxpr/ppermute | solution.py:15
  213.0 9.9 %collective-permute-start.1 = (f32[2,16,1,256]{3,2,1,0:T(1,128)S(1)}, f32[2,16,1,256]{3,2,1,0:T(1,128)S(1)}, u32[]{:S(2)}, u32[]{:S(2)}) collective-permute-start(f32[2,16,1,256]{3,2,1,0:T(1,128)S(1)} %pad_maximum_fusion.11), channel_id=1, source_target_pairs={{1,0},{2,1},{3,2},{4,3},{5,4},{6,5},{7,6},{9,8},{10,9},{11,10},{12... | collective-permute-start | bytes 98312 | tf_op jit(solution)/shard_map/while/body/eval_jaxpr/ppermute | solution.py:15
  214.3 8.5 %collective-permute-start = (f32[2,1,16,256]{3,2,1,0:T(8,128)S(1)}, f32[2,1,16,256]{3,2,1,0:T(8,128)S(1)}, u32[]{:S(2)}, u32[]{:S(2)}) collective-permute-start(f32[2,1,16,256]{3,2,1,0:T(8,128)S(1)} %pad_maximum_fusion.10), channel_id=1, source_target_pairs={{8,0},{16,8},{24,16},{9,1},{17,9},{25,17},{10,2},{18,10},{26,18},{... | collective-permute-start | bytes 98312 | tf_op jit(solution)/shard_map/while/body/eval_jaxpr/ppermute | solution.py:15
  225.9 12.4 %collective-permute-start.2 = (f32[2,16,1,256]{3,2,1,0:T(1,128)S(1)}, f32[2,16,1,256]{3,2,1,0:T(1,128)S(1)}, u32[]{:S(2)}, u32[]{:S(2)}) collective-permute-start(f32[2,16,1,256]{3,2,1,0:T(1,128)S(1)} %pad_maximum_fusion.12), channel_id=1, source_target_pairs={{0,1},{1,2},{2,3},{3,4},{4,5},{5,6},{6,7},{8,9},{9,10},{10,11},{11... | collective-permute-start | bytes 98312 | tf_op jit(solution)/shard_map/while/body/eval_jaxpr/ppermute | solution.py:15
  233.0 6.1 %collective-permute-start.3 = (f32[2,1,16,256]{3,2,1,0:T(8,128)S(1)}, f32[2,1,16,256]{3,2,1,0:T(8,128)S(1)}, u32[]{:S(2)}, u32[]{:S(2)}) collective-permute-start(f32[2,1,16,256]{3,2,1,0:T(8,128)S(1)} %pad_maximum_fusion.13), channel_id=1, source_target_pairs={{0,8},{8,16},{16,24},{1,9},{9,17},{17,25},{2,10},{10,18},{18,26},{... | collective-permute-start | bytes 98312 | tf_op jit(solution)/shard_map/while/body/eval_jaxpr/ppermute | solution.py:15
  247.3 9.9 %collective-permute-start.1 = (f32[2,16,1,256]{3,2,1,0:T(1,128)S(1)}, f32[2,16,1,256]{3,2,1,0:T(1,128)S(1)}, u32[]{:S(2)}, u32[]{:S(2)}) collective-permute-start(f32[2,16,1,256]{3,2,1,0:T(1,128)S(1)} %pad_maximum_fusion.11), channel_id=1, source_target_pairs={{1,0},{2,1},{3,2},{4,3},{5,4},{6,5},{7,6},{9,8},{10,9},{11,10},{12... | collective-permute-start | bytes 98312 | tf_op jit(solution)/shard_map/while/body/eval_jaxpr/ppermute | solution.py:15
  248.6 8.5 %collective-permute-start = (f32[2,1,16,256]{3,2,1,0:T(8,128)S(1)}, f32[2,1,16,256]{3,2,1,0:T(8,128)S(1)}, u32[]{:S(2)}, u32[]{:S(2)}) collective-permute-start(f32[2,1,16,256]{3,2,1,0:T(8,128)S(1)} %pad_maximum_fusion.10), channel_id=1, source_target_pairs={{8,0},{16,8},{24,16},{9,1},{17,9},{25,17},{10,2},{18,10},{26,18},{... | collective-permute-start | bytes 98312 | tf_op jit(solution)/shard_map/while/body/eval_jaxpr/ppermute | solution.py:15
  260.2 12.4 %collective-permute-start.2 = (f32[2,16,1,256]{3,2,1,0:T(1,128)S(1)}, f32[2,16,1,256]{3,2,1,0:T(1,128)S(1)}, u32[]{:S(2)}, u32[]{:S(2)}) collective-permute-start(f32[2,16,1,256]{3,2,1,0:T(1,128)S(1)} %pad_maximum_fusion.12), channel_id=1, source_target_pairs={{0,1},{1,2},{2,3},{3,4},{4,5},{5,6},{6,7},{8,9},{9,10},{10,11},{11... | collective-permute-start | bytes 98312 | tf_op jit(solution)/shard_map/while/body/eval_jaxpr/ppermute | solution.py:15
  267.3 6.1 %collective-permute-start.3 = (f32[2,1,16,256]{3,2,1,0:T(8,128)S(1)}, f32[2,1,16,256]{3,2,1,0:T(8,128)S(1)}, u32[]{:S(2)}, u32[]{:S(2)}) collective-permute-start(f32[2,1,16,256]{3,2,1,0:T(8,128)S(1)} %pad_maximum_fusion.13), channel_id=1, source_target_pairs={{0,8},{8,16},{16,24},{1,9},{9,17},{17,25},{2,10},{10,18},{18,26},{... | collective-permute-start | bytes 98312 | tf_op jit(solution)/shard_map/while/body/eval_jaxpr/ppermute | solution.py:15
  281.6 9.9 %collective-permute-start.1 = (f32[2,16,1,256]{3,2,1,0:T(1,128)S(1)}, f32[2,16,1,256]{3,2,1,0:T(1,128)S(1)}, u32[]{:S(2)}, u32[]{:S(2)}) collective-permute-start(f32[2,16,1,256]{3,2,1,0:T(1,128)S(1)} %pad_maximum_fusion.11), channel_id=1, source_target_pairs={{1,0},{2,1},{3,2},{4,3},{5,4},{6,5},{7,6},{9,8},{10,9},{11,10},{12... | collective-permute-start | bytes 98312 | tf_op jit(solution)/shard_map/while/body/eval_jaxpr/ppermute | solution.py:15
  282.9 8.5 %collective-permute-start = (f32[2,1,16,256]{3,2,1,0:T(8,128)S(1)}, f32[2,1,16,256]{3,2,1,0:T(8,128)S(1)}, u32[]{:S(2)}, u32[]{:S(2)}) collective-permute-start(f32[2,1,16,256]{3,2,1,0:T(8,128)S(1)} %pad_maximum_fusion.10), channel_id=1, source_target_pairs={{8,0},{16,8},{24,16},{9,1},{17,9},{25,17},{10,2},{18,10},{26,18},{... | collective-permute-start | bytes 98312 | tf_op jit(solution)/shard_map/while/body/eval_jaxpr/ppermute | solution.py:15
  294.5 12.4 %collective-permute-start.2 = (f32[2,16,1,256]{3,2,1,0:T(1,128)S(1)}, f32[2,16,1,256]{3,2,1,0:T(1,128)S(1)}, u32[]{:S(2)}, u32[]{:S(2)}) collective-permute-start(f32[2,16,1,256]{3,2,1,0:T(1,128)S(1)} %pad_maximum_fusion.12), channel_id=1, source_target_pairs={{0,1},{1,2},{2,3},{3,4},{4,5},{5,6},{6,7},{8,9},{9,10},{10,11},{11... | collective-permute-start | bytes 98312 | tf_op jit(solution)/shard_map/while/body/eval_jaxpr/ppermute | solution.py:15
  301.6 6.1 %collective-permute-start.3 = (f32[2,1,16,256]{3,2,1,0:T(8,128)S(1)}, f32[2,1,16,256]{3,2,1,0:T(8,128)S(1)}, u32[]{:S(2)}, u32[]{:S(2)}) collective-permute-start(f32[2,1,16,256]{3,2,1,0:T(8,128)S(1)} %pad_maximum_fusion.13), channel_id=1, source_target_pairs={{0,8},{8,16},{16,24},{1,9},{9,17},{17,25},{2,10},{10,18},{18,26},{... | collective-permute-start | bytes 98312 | tf_op jit(solution)/shard_map/while/body/eval_jaxpr/ppermute | solution.py:15
  315.9 9.9 %collective-permute-start.1 = (f32[2,16,1,256]{3,2,1,0:T(1,128)S(1)}, f32[2,16,1,256]{3,2,1,0:T(1,128)S(1)}, u32[]{:S(2)}, u32[]{:S(2)}) collective-permute-start(f32[2,16,1,256]{3,2,1,0:T(1,128)S(1)} %pad_maximum_fusion.11), channel_id=1, source_target_pairs={{1,0},{2,1},{3,2},{4,3},{5,4},{6,5},{7,6},{9,8},{10,9},{11,10},{12... | collective-permute-start | bytes 98312 | tf_op jit(solution)/shard_map/while/body/eval_jaxpr/ppermute | solution.py:15
  317.2 8.5 %collective-permute-start = (f32[2,1,16,256]{3,2,1,0:T(8,128)S(1)}, f32[2,1,16,256]{3,2,1,0:T(8,128)S(1)}, u32[]{:S(2)}, u32[]{:S(2)}) collective-permute-start(f32[2,1,16,256]{3,2,1,0:T(8,128)S(1)} %pad_maximum_fusion.10), channel_id=1, source_target_pairs={{8,0},{16,8},{24,16},{9,1},{17,9},{25,17},{10,2},{18,10},{26,18},{... | collective-permute-start | bytes 98312 | tf_op jit(solution)/shard_map/while/body/eval_jaxpr/ppermute | solution.py:15
  328.8 12.4 %collective-permute-start.2 = (f32[2,16,1,256]{3,2,1,0:T(1,128)S(1)}, f32[2,16,1,256]{3,2,1,0:T(1,128)S(1)}, u32[]{:S(2)}, u32[]{:S(2)}) collective-permute-start(f32[2,16,1,256]{3,2,1,0:T(1,128)S(1)} %pad_maximum_fusion.12), channel_id=1, source_target_pairs={{0,1},{1,2},{2,3},{3,4},{4,5},{5,6},{6,7},{8,9},{9,10},{10,11},{11... | collective-permute-start | bytes 98312 | tf_op jit(solution)/shard_map/while/body/eval_jaxpr/ppermute | solution.py:15
  335.9 6.1 %collective-permute-start.3 = (f32[2,1,16,256]{3,2,1,0:T(8,128)S(1)}, f32[2,1,16,256]{3,2,1,0:T(8,128)S(1)}, u32[]{:S(2)}, u32[]{:S(2)}) collective-permute-start(f32[2,1,16,256]{3,2,1,0:T(8,128)S(1)} %pad_maximum_fusion.13), channel_id=1, source_target_pairs={{0,8},{8,16},{16,24},{1,9},{9,17},{17,25},{2,10},{10,18},{18,26},{... | collective-permute-start | bytes 98312 | tf_op jit(solution)/shard_map/while/body/eval_jaxpr/ppermute | solution.py:15
  350.2 9.9 %collective-permute-start.1 = (f32[2,16,1,256]{3,2,1,0:T(1,128)S(1)}, f32[2,16,1,256]{3,2,1,0:T(1,128)S(1)}, u32[]{:S(2)}, u32[]{:S(2)}) collective-permute-start(f32[2,16,1,256]{3,2,1,0:T(1,128)S(1)} %pad_maximum_fusion.11), channel_id=1, source_target_pairs={{1,0},{2,1},{3,2},{4,3},{5,4},{6,5},{7,6},{9,8},{10,9},{11,10},{12... | collective-permute-start | bytes 98312 | tf_op jit(solution)/shard_map/while/body/eval_jaxpr/ppermute | solution.py:15
  351.5 8.5 %collective-permute-start = (f32[2,1,16,256]{3,2,1,0:T(8,128)S(1)}, f32[2,1,16,256]{3,2,1,0:T(8,128)S(1)}, u32[]{:S(2)}, u32[]{:S(2)}) collective-permute-start(f32[2,1,16,256]{3,2,1,0:T(8,128)S(1)} %pad_maximum_fusion.10), channel_id=1, source_target_pairs={{8,0},{16,8},{24,16},{9,1},{17,9},{25,17},{10,2},{18,10},{26,18},{... | collective-permute-start | bytes 98312 | tf_op jit(solution)/shard_map/while/body/eval_jaxpr/ppermute | solution.py:15
  363.1 12.4 %collective-permute-start.2 = (f32[2,16,1,256]{3,2,1,0:T(1,128)S(1)}, f32[2,16,1,256]{3,2,1,0:T(1,128)S(1)}, u32[]{:S(2)}, u32[]{:S(2)}) collective-permute-start(f32[2,16,1,256]{3,2,1,0:T(1,128)S(1)} %pad_maximum_fusion.12), channel_id=1, source_target_pairs={{0,1},{1,2},{2,3},{3,4},{4,5},{5,6},{6,7},{8,9},{9,10},{10,11},{11... | collective-permute-start | bytes 98312 | tf_op jit(solution)/shard_map/while/body/eval_jaxpr/ppermute | solution.py:15
  370.2 6.1 %collective-permute-start.3 = (f32[2,1,16,256]{3,2,1,0:T(8,128)S(1)}, f32[2,1,16,256]{3,2,1,0:T(8,128)S(1)}, u32[]{:S(2)}, u32[]{:S(2)}) collective-permute-start(f32[2,1,16,256]{3,2,1,0:T(8,128)S(1)} %pad_maximum_fusion.13), channel_id=1, source_target_pairs={{0,8},{8,16},{16,24},{1,9},{9,17},{17,25},{2,10},{10,18},{18,26},{... | collective-permute-start | bytes 98312 | tf_op jit(solution)/shard_map/while/body/eval_jaxpr/ppermute | solution.py:15
  384.5 9.9 %collective-permute-start.1 = (f32[2,16,1,256]{3,2,1,0:T(1,128)S(1)}, f32[2,16,1,256]{3,2,1,0:T(1,128)S(1)}, u32[]{:S(2)}, u32[]{:S(2)}) collective-permute-start(f32[2,16,1,256]{3,2,1,0:T(1,128)S(1)} %pad_maximum_fusion.11), channel_id=1, source_target_pairs={{1,0},{2,1},{3,2},{4,3},{5,4},{6,5},{7,6},{9,8},{10,9},{11,10},{12... | collective-permute-start | bytes 98312 | tf_op jit(solution)/shard_map/while/body/eval_jaxpr/ppermute | solution.py:15
  385.8 8.5 %collective-permute-start = (f32[2,1,16,256]{3,2,1,0:T(8,128)S(1)}, f32[2,1,16,256]{3,2,1,0:T(8,128)S(1)}, u32[]{:S(2)}, u32[]{:S(2)}) collective-permute-start(f32[2,1,16,256]{3,2,1,0:T(8,128)S(1)} %pad_maximum_fusion.10), channel_id=1, source_target_pairs={{8,0},{16,8},{24,16},{9,1},{17,9},{25,17},{10,2},{18,10},{26,18},{... | collective-permute-start | bytes 98312 | tf_op jit(solution)/shard_map/while/body/eval_jaxpr/ppermute | solution.py:15
  397.4 12.4 %collective-permute-start.2 = (f32[2,16,1,256]{3,2,1,0:T(1,128)S(1)}, f32[2,16,1,256]{3,2,1,0:T(1,128)S(1)}, u32[]{:S(2)}, u32[]{:S(2)}) collective-permute-start(f32[2,16,1,256]{3,2,1,0:T(1,128)S(1)} %pad_maximum_fusion.12), channel_id=1, source_target_pairs={{0,1},{1,2},{2,3},{3,4},{4,5},{5,6},{6,7},{8,9},{9,10},{10,11},{11... | collective-permute-start | bytes 98312 | tf_op jit(solution)/shard_map/while/body/eval_jaxpr/ppermute | solution.py:15
  404.5 6.1 %collective-permute-start.3 = (f32[2,1,16,256]{3,2,1,0:T(8,128)S(1)}, f32[2,1,16,256]{3,2,1,0:T(8,128)S(1)}, u32[]{:S(2)}, u32[]{:S(2)}) collective-permute-start(f32[2,1,16,256]{3,2,1,0:T(8,128)S(1)} %pad_maximum_fusion.13), channel_id=1, source_target_pairs={{0,8},{8,16},{16,24},{1,9},{9,17},{17,25},{2,10},{10,18},{18,26},{... | collective-permute-start | bytes 98312 | tf_op jit(solution)/shard_map/while/body/eval_jaxpr/ppermute | solution.py:15
  418.8 9.9 %collective-permute-start.1 = (f32[2,16,1,256]{3,2,1,0:T(1,128)S(1)}, f32[2,16,1,256]{3,2,1,0:T(1,128)S(1)}, u32[]{:S(2)}, u32[]{:S(2)}) collective-permute-start(f32[2,16,1,256]{3,2,1,0:T(1,128)S(1)} %pad_maximum_fusion.11), channel_id=1, source_target_pairs={{1,0},{2,1},{3,2},{4,3},{5,4},{6,5},{7,6},{9,8},{10,9},{11,10},{12... | collective-permute-start | bytes 98312 | tf_op jit(solution)/shard_map/while/body/eval_jaxpr/ppermute | solution.py:15
  420.1 8.5 %collective-permute-start = (f32[2,1,16,256]{3,2,1,0:T(8,128)S(1)}, f32[2,1,16,256]{3,2,1,0:T(8,128)S(1)}, u32[]{:S(2)}, u32[]{:S(2)}) collective-permute-start(f32[2,1,16,256]{3,2,1,0:T(8,128)S(1)} %pad_maximum_fusion.10), channel_id=1, source_target_pairs={{8,0},{16,8},{24,16},{9,1},{17,9},{25,17},{10,2},{18,10},{26,18},{... | collective-permute-start | bytes 98312 | tf_op jit(solution)/shard_map/while/body/eval_jaxpr/ppermute | solution.py:15
  431.7 12.4 %collective-permute-start.2 = (f32[2,16,1,256]{3,2,1,0:T(1,128)S(1)}, f32[2,16,1,256]{3,2,1,0:T(1,128)S(1)}, u32[]{:S(2)}, u32[]{:S(2)}) collective-permute-start(f32[2,16,1,256]{3,2,1,0:T(1,128)S(1)} %pad_maximum_fusion.12), channel_id=1, source_target_pairs={{0,1},{1,2},{2,3},{3,4},{4,5},{5,6},{6,7},{8,9},{9,10},{10,11},{11... | collective-permute-start | bytes 98312 | tf_op jit(solution)/shard_map/while/body/eval_jaxpr/ppermute | solution.py:15
  438.8 6.1 %collective-permute-start.3 = (f32[2,1,16,256]{3,2,1,0:T(8,128)S(1)}, f32[2,1,16,256]{3,2,1,0:T(8,128)S(1)}, u32[]{:S(2)}, u32[]{:S(2)}) collective-permute-start(f32[2,1,16,256]{3,2,1,0:T(8,128)S(1)} %pad_maximum_fusion.13), channel_id=1, source_target_pairs={{0,8},{8,16},{16,24},{1,9},{9,17},{17,25},{2,10},{10,18},{18,26},{... | collective-permute-start | bytes 98312 | tf_op jit(solution)/shard_map/while/body/eval_jaxpr/ppermute | solution.py:15
  453.1 9.9 %collective-permute-start.1 = (f32[2,16,1,256]{3,2,1,0:T(1,128)S(1)}, f32[2,16,1,256]{3,2,1,0:T(1,128)S(1)}, u32[]{:S(2)}, u32[]{:S(2)}) collective-permute-start(f32[2,16,1,256]{3,2,1,0:T(1,128)S(1)} %pad_maximum_fusion.11), channel_id=1, source_target_pairs={{1,0},{2,1},{3,2},{4,3},{5,4},{6,5},{7,6},{9,8},{10,9},{11,10},{12... | collective-permute-start | bytes 98312 | tf_op jit(solution)/shard_map/while/body/eval_jaxpr/ppermute | solution.py:15
  454.4 8.5 %collective-permute-start = (f32[2,1,16,256]{3,2,1,0:T(8,128)S(1)}, f32[2,1,16,256]{3,2,1,0:T(8,128)S(1)}, u32[]{:S(2)}, u32[]{:S(2)}) collective-permute-start(f32[2,1,16,256]{3,2,1,0:T(8,128)S(1)} %pad_maximum_fusion.10), channel_id=1, source_target_pairs={{8,0},{16,8},{24,16},{9,1},{17,9},{25,17},{10,2},{18,10},{26,18},{... | collective-permute-start | bytes 98312 | tf_op jit(solution)/shard_map/while/body/eval_jaxpr/ppermute | solution.py:15
  466.0 12.4 %collective-permute-start.2 = (f32[2,16,1,256]{3,2,1,0:T(1,128)S(1)}, f32[2,16,1,256]{3,2,1,0:T(1,128)S(1)}, u32[]{:S(2)}, u32[]{:S(2)}) collective-permute-start(f32[2,16,1,256]{3,2,1,0:T(1,128)S(1)} %pad_maximum_fusion.12), channel_id=1, source_target_pairs={{0,1},{1,2},{2,3},{3,4},{4,5},{5,6},{6,7},{8,9},{9,10},{10,11},{11... | collective-permute-start | bytes 98312 | tf_op jit(solution)/shard_map/while/body/eval_jaxpr/ppermute | solution.py:15
  473.1 6.1 %collective-permute-start.3 = (f32[2,1,16,256]{3,2,1,0:T(8,128)S(1)}, f32[2,1,16,256]{3,2,1,0:T(8,128)S(1)}, u32[]{:S(2)}, u32[]{:S(2)}) collective-permute-start(f32[2,1,16,256]{3,2,1,0:T(8,128)S(1)} %pad_maximum_fusion.13), channel_id=1, source_target_pairs={{0,8},{8,16},{16,24},{1,9},{9,17},{17,25},{2,10},{10,18},{18,26},{... | collective-permute-start | bytes 98312 | tf_op jit(solution)/shard_map/while/body/eval_jaxpr/ppermute | solution.py:15
  487.4 9.9 %collective-permute-start.1 = (f32[2,16,1,256]{3,2,1,0:T(1,128)S(1)}, f32[2,16,1,256]{3,2,1,0:T(1,128)S(1)}, u32[]{:S(2)}, u32[]{:S(2)}) collective-permute-start(f32[2,16,1,256]{3,2,1,0:T(1,128)S(1)} %pad_maximum_fusion.11), channel_id=1, source_target_pairs={{1,0},{2,1},{3,2},{4,3},{5,4},{6,5},{7,6},{9,8},{10,9},{11,10},{12... | collective-permute-start | bytes 98312 | tf_op jit(solution)/shard_map/while/body/eval_jaxpr/ppermute | solution.py:15
  488.7 8.5 %collective-permute-start = (f32[2,1,16,256]{3,2,1,0:T(8,128)S(1)}, f32[2,1,16,256]{3,2,1,0:T(8,128)S(1)}, u32[]{:S(2)}, u32[]{:S(2)}) collective-permute-start(f32[2,1,16,256]{3,2,1,0:T(8,128)S(1)} %pad_maximum_fusion.10), channel_id=1, source_target_pairs={{8,0},{16,8},{24,16},{9,1},{17,9},{25,17},{10,2},{18,10},{26,18},{... | collective-permute-start | bytes 98312 | tf_op jit(solution)/shard_map/while/body/eval_jaxpr/ppermute | solution.py:15
  500.3 12.4 %collective-permute-start.2 = (f32[2,16,1,256]{3,2,1,0:T(1,128)S(1)}, f32[2,16,1,256]{3,2,1,0:T(1,128)S(1)}, u32[]{:S(2)}, u32[]{:S(2)}) collective-permute-start(f32[2,16,1,256]{3,2,1,0:T(1,128)S(1)} %pad_maximum_fusion.12), channel_id=1, source_target_pairs={{0,1},{1,2},{2,3},{3,4},{4,5},{5,6},{6,7},{8,9},{9,10},{10,11},{11... | collective-permute-start | bytes 98312 | tf_op jit(solution)/shard_map/while/body/eval_jaxpr/ppermute | solution.py:15
  507.4 6.1 %collective-permute-start.3 = (f32[2,1,16,256]{3,2,1,0:T(8,128)S(1)}, f32[2,1,16,256]{3,2,1,0:T(8,128)S(1)}, u32[]{:S(2)}, u32[]{:S(2)}) collective-permute-start(f32[2,1,16,256]{3,2,1,0:T(8,128)S(1)} %pad_maximum_fusion.13), channel_id=1, source_target_pairs={{0,8},{8,16},{16,24},{1,9},{9,17},{17,25},{2,10},{10,18},{18,26},{... | collective-permute-start | bytes 98312 | tf_op jit(solution)/shard_map/while/body/eval_jaxpr/ppermute | solution.py:15
  521.7 9.9 %collective-permute-start.1 = (f32[2,16,1,256]{3,2,1,0:T(1,128)S(1)}, f32[2,16,1,256]{3,2,1,0:T(1,128)S(1)}, u32[]{:S(2)}, u32[]{:S(2)}) collective-permute-start(f32[2,16,1,256]{3,2,1,0:T(1,128)S(1)} %pad_maximum_fusion.11), channel_id=1, source_target_pairs={{1,0},{2,1},{3,2},{4,3},{5,4},{6,5},{7,6},{9,8},{10,9},{11,10},{12... | collective-permute-start | bytes 98312 | tf_op jit(solution)/shard_map/while/body/eval_jaxpr/ppermute | solution.py:15
  523.0 8.5 %collective-permute-start = (f32[2,1,16,256]{3,2,1,0:T(8,128)S(1)}, f32[2,1,16,256]{3,2,1,0:T(8,128)S(1)}, u32[]{:S(2)}, u32[]{:S(2)}) collective-permute-start(f32[2,1,16,256]{3,2,1,0:T(8,128)S(1)} %pad_maximum_fusion.10), channel_id=1, source_target_pairs={{8,0},{16,8},{24,16},{9,1},{17,9},{25,17},{10,2},{18,10},{26,18},{... | collective-permute-start | bytes 98312 | tf_op jit(solution)/shard_map/while/body/eval_jaxpr/ppermute | solution.py:15
  534.6 12.4 %collective-permute-start.2 = (f32[2,16,1,256]{3,2,1,0:T(1,128)S(1)}, f32[2,16,1,256]{3,2,1,0:T(1,128)S(1)}, u32[]{:S(2)}, u32[]{:S(2)}) collective-permute-start(f32[2,16,1,256]{3,2,1,0:T(1,128)S(1)} %pad_maximum_fusion.12), channel_id=1, source_target_pairs={{0,1},{1,2},{2,3},{3,4},{4,5},{5,6},{6,7},{8,9},{9,10},{10,11},{11... | collective-permute-start | bytes 98312 | tf_op jit(solution)/shard_map/while/body/eval_jaxpr/ppermute | solution.py:15
  541.7 6.1 %collective-permute-start.3 = (f32[2,1,16,256]{3,2,1,0:T(8,128)S(1)}, f32[2,1,16,256]{3,2,1,0:T(8,128)S(1)}, u32[]{:S(2)}, u32[]{:S(2)}) collective-permute-start(f32[2,1,16,256]{3,2,1,0:T(8,128)S(1)} %pad_maximum_fusion.13), channel_id=1, source_target_pairs={{0,8},{8,16},{16,24},{1,9},{9,17},{17,25},{2,10},{10,18},{18,26},{... | collective-permute-start | bytes 98312 | tf_op jit(solution)/shard_map/while/body/eval_jaxpr/ppermute | solution.py:15
  (424 other events, 2364.7 us)
where the time goes:
time: 612 us; the launch traced here: 605 us
  starting transfers between devices  205 us (33%)
  local copies, waits for them, and re-layouts  160 us (26%)
  other arithmetic  119 us (19%)
  matrix products  52.2 us (9%)
  blocking collectives  45.9 us (8%)
  waiting for transfers between devices  13.2 us (2%)
  loops' own time  7.44 us (1%)
    ppermute x64, starting transfers between devices, passed_along(): return lax.ppermute(block, axis, route)  205 us
    slice x96, local copies, waits for them, and re-layouts, difference(): lax.slice_in_dim(values, 1, length, axis=axis)  73.3 us
    sub x48, other arithmetic, turn_parts(): field_h[number] - courant * rotation[number]  50.2 us
    psum x1, blocking collectives, local(): port_power = lax.psum(partial_value, ('gx', 'gy'))  45.9 us
    add x16, other arithmetic, turn_parts(): field_e[1] + factor * rotation[1]  38.7 us
    while x832, local copies, waits for them, and re-layouts  36.9 us
    dot_general x16, matrix products, inject(): lax.dot_general(weighted, depth_table, (((0,), (0,)), ((), ())), precisio...  30.5 us
    dynamic_update_slice x16, local copies, waits for them, and re-layouts, note_power(): return lax.dynamic_update_slice_in_dim(record, drive[None, :], index, 0)  21.4 us
  transfers between devices with their start and end apart: 64, of which 16 were waited for; matrix products, arithmetic and copies ran while one was open for 22% of the time, Pallas kernels for 0%

commit v1 on v0

--- a/solution.py
+++ b/solution.py
@@ -134,7 +134,7 @@
     electric = jnp.stack(parts_e)
     magnetic = jnp.stack(parts_h)
     partial_value = jnp.dot(record, members, precision=lax.Precision.HIGHEST)
-    port_power = lax.psum(partial_value, ("gx", "gy"))
+    port_power = lax.psum(lax.psum(partial_value, "gx"), "gy")
     return (electric, magnetic, port_power)
 
 

time: 612 us -> 616 us (level)
    psum x1 -> x2, blocking collectives: 45.9 us -> 49.6 us  [local(): port_power = lax.psum(lax.psum(partial_value, 'gx'), 'gy')]
where the time goes in v1:
time: 616 us; the launch traced here: 610 us
  starting transfers between devices  205 us (33%)
  local copies, waits for them, and re-layouts  161 us (26%)
  other arithmetic  120 us (19%)
  matrix products  52.3 us (8%)
  blocking collectives  49.6 us (8%)
  waiting for transfers between devices  13.2 us (2%)
  loops' own time  7.44 us (1%)
    ppermute x64, starting transfers between devices, passed_along(): return lax.ppermute(block, axis, route)  205 us
    slice x96, local copies, waits for them, and re-layouts, difference(): lax.slice_in_dim(values, 1, length, axis=axis)  73.8 us
    sub x48, other arithmetic, turn_parts(): field_h[number] - courant * rotation[number]  50.8 us
    psum x2, blocking collectives, local(): port_power = lax.psum(lax.psum(partial_value, 'gx'), 'gy')  49.6 us
    add x16, other arithmetic, turn_parts(): field_e[1] + factor * rotation[1]  39 us
    while x832, local copies, waits for them, and re-layouts  36.9 us
    dot_general x16, matrix products, inject(): lax.dot_general(weighted, depth_table, (((0,), (0,)), ((), ())), precisio...  30.6 us
    dynamic_update_slice x16, local copies, waits for them, and re-layouts, note_power(): return lax.dynamic_update_slice_in_dim(record, drive[None, :], index, 0)  21.4 us
  transfers between devices with their start and end apart: 64, of which 16 were waited for; matrix products, arithmetic and copies ran while one was open for 22% of the time, Pallas kernels for 0%

profile of v1, /device:TPU:0, one launch (start us, length us, event | category | flops | bytes accessed | tf_op | source)
XLA Modules:
  0.0 609.9 jit_solution(16773848233371251133)
XLA Ops:
  10.6 546.5 %while.50 = (s32[]{:T(128)}, f32[16,16,256]{2,1,0:T(8,128)S(1)}, f32[16,16,256]{2,1,0:T(8,128)S(1)}, f32[16,16,256]{2,1,0:T(8,128)S(1)}, f32[16,16,256]{2,1,0:T(...) while((s32[]{:T(128)}, f32[16,16,256]{2,1,0:T(8,128)S(1)}, ...), condition=%wide.region_2.3_spmd.clone, body=%wide.region_0.2_spmd.clone.sunk | while | flops 812285952 | bytes 56044672 | solution.py:133
  20.6 2.5 multiply_subtract_fusion.7
  23.6 5.5 collective-permute-start.2
  31.0 2.8 collective-permute-start.3
  39.2 2.4 multiply_add_fusion.5
  52.8 2.5 multiply_subtract_fusion.7
  55.8 5.5 collective-permute-start.2
  63.2 3.8 collective-permute-start.3
  72.3 2.4 multiply_add_fusion.5
  86.0 2.5 multiply_subtract_fusion.7
  89.0 5.2 collective-permute-start.2
  96.0 5.3 collective-permute-start.3
  106.7 2.4 multiply_add_fusion.5
  120.3 2.5 multiply_subtract_fusion.7
  123.4 5.2 collective-permute-start.2
  130.4 5.3 collective-permute-start.3
  141.1 2.4 multiply_add_fusion.5
  154.7 2.5 multiply_subtract_fusion.7
  157.7 5.2 collective-permute-start.2
  164.8 5.3 collective-permute-start.3
  175.5 2.4 multiply_add_fusion.5
  189.1 2.5 multiply_subtract_fusion.7
  192.1 5.2 collective-permute-start.2
  199.2 5.3 collective-permute-start.3
  209.8 2.4 multiply_add_fusion.5
  223.4 2.5 multiply_subtract_fusion.7
  226.5 5.2 collective-permute-start.2
  233.5 5.3 collective-permute-start.3
  244.2 2.4 multiply_add_fusion.5
  257.8 2.5 multiply_subtract_fusion.7
  260.8 5.2 collective-permute-start.2
  267.9 5.3 collective-permute-start.3
  278.6 2.4 multiply_add_fusion.5
  292.2 2.5 multiply_subtract_fusion.7
  295.2 5.2 collective-permute-start.2
  302.3 5.3 collective-permute-start.3
  312.9 2.4 multiply_add_fusion.5
  326.6 2.5 multiply_subtract_fusion.7
  329.6 5.2 collective-permute-start.2
  336.6 5.3 collective-permute-start.3
  347.3 2.4 multiply_add_fusion.5
  360.9 2.5 multiply_subtract_fusion.7
  364.0 5.2 collective-permute-start.2
  371.0 5.3 collective-permute-start.3
  395.3 2.5 multiply_subtract_fusion.7
  398.3 5.2 collective-permute-start.2
  405.4 5.3 collective-permute-start.3
  429.7 2.5 multiply_subtract_fusion.7
  432.7 5.2 collective-permute-start.2
  439.7 5.3 collective-permute-start.3
  450.4 2.4 multiply_add_fusion.5
  464.0 2.5 multiply_subtract_fusion.7
  467.1 5.2 collective-permute-start.2
  474.1 5.3 collective-permute-start.3
  484.8 2.4 multiply_add_fusion.5
  498.4 2.5 multiply_subtract_fusion.7
  501.4 5.2 collective-permute-start.2
  508.5 5.3 collective-permute-start.3
  519.2 2.4 multiply_add_fusion.5
  532.8 2.5 multiply_subtract_fusion.7
  535.8 5.2 collective-permute-start.2
  542.9 5.3 collective-permute-start.3
  558.4 13.0 %psum.14 = f32[16,512]{1,0:T(8,128)S(1)} all-reduce(f32[16,512]{1,0:T(8,128)S(1)} %fusion.27), channel_id=1, replica_groups=mesh['gx'=4,'gy'=8] {'gx'}, use_global_device_ids=true, to_apply=%region_3.4 | all-reduce | flops 8192 | bytes 65536 | tf_op jit(solution)/shard_map/psum | solution.py:137
  571.4 36.6 %psum.15 = f32[16,512]{1,0:T(8,128)} all-reduce(f32[16,512]{1,0:T(8,128)S(1)} %psum.14), channel_id=1, replica_groups=mesh['gx'=4,'gy'=8] {'gy'}, use_global_device_ids=true, to_apply=%region_4.5 | all-reduce | flops 8192 | bytes 65536 | tf_op jit(solution)/shard_map/psum | solution.py:137
  (1455 shorter events, 316.2 us)
Async XLA Ops:
  10.7 9.9 %collective-permute-start.1 = (f32[2,16,1,256]{3,2,1,0:T(1,128)S(1)}, f32[2,16,1,256]{3,2,1,0:T(1,128)S(1)}, u32[]{:S(2)}, u32[]{:S(2)}) collective-permute-start(f32[2,16,1,256]{3,2,1,0:T(1,128)S(1)} %pad_maximum_fusion.11), channel_id=1, source_target_pairs={{1,0},{2,1},{3,2},{4,3},{5,4},{6,5},{7,6},{9,8},{10,9},{11,10},{12... | collective-permute-start | bytes 98312 | tf_op jit(solution)/shard_map/while/body/eval_jaxpr/ppermute | solution.py:15
  12.0 8.6 %collective-permute-start = (f32[2,1,16,256]{3,2,1,0:T(8,128)S(1)}, f32[2,1,16,256]{3,2,1,0:T(8,128)S(1)}, u32[]{:S(2)}, u32[]{:S(2)}) collective-permute-start(f32[2,1,16,256]{3,2,1,0:T(8,128)S(1)} %pad_maximum_fusion.10), channel_id=1, source_target_pairs={{8,0},{16,8},{24,16},{9,1},{17,9},{25,17},{10,2},{18,10},{26,18},{... | collective-permute-start | bytes 98312 | tf_op jit(solution)/shard_map/while/body/eval_jaxpr/ppermute | solution.py:15
  23.6 10.2 %collective-permute-start.2 = (f32[2,16,1,256]{3,2,1,0:T(1,128)S(1)}, f32[2,16,1,256]{3,2,1,0:T(1,128)S(1)}, u32[]{:S(2)}, u32[]{:S(2)}) collective-permute-start(f32[2,16,1,256]{3,2,1,0:T(1,128)S(1)} %pad_maximum_fusion.12), channel_id=1, source_target_pairs={{0,1},{1,2},{2,3},{3,4},{4,5},{5,6},{6,7},{8,9},{9,10},{10,11},{11... | collective-permute-start | bytes 98312 | tf_op jit(solution)/shard_map/while/body/eval_jaxpr/ppermute | solution.py:15
  31.0 3.6 collective-permute-start.3
  42.9 9.9 %collective-permute-start.1 = (f32[2,16,1,256]{3,2,1,0:T(1,128)S(1)}, f32[2,16,1,256]{3,2,1,0:T(1,128)S(1)}, u32[]{:S(2)}, u32[]{:S(2)}) collective-permute-start(f32[2,16,1,256]{3,2,1,0:T(1,128)S(1)} %pad_maximum_fusion.11), channel_id=1, source_target_pairs={{1,0},{2,1},{3,2},{4,3},{5,4},{6,5},{7,6},{9,8},{10,9},{11,10},{12... | collective-permute-start | bytes 98312 | tf_op jit(solution)/shard_map/while/body/eval_jaxpr/ppermute | solution.py:15
  44.2 8.6 %collective-permute-start = (f32[2,1,16,256]{3,2,1,0:T(8,128)S(1)}, f32[2,1,16,256]{3,2,1,0:T(8,128)S(1)}, u32[]{:S(2)}, u32[]{:S(2)}) collective-permute-start(f32[2,1,16,256]{3,2,1,0:T(8,128)S(1)} %pad_maximum_fusion.10), channel_id=1, source_target_pairs={{8,0},{16,8},{24,16},{9,1},{17,9},{25,17},{10,2},{18,10},{26,18},{... | collective-permute-start | bytes 98312 | tf_op jit(solution)/shard_map/while/body/eval_jaxpr/ppermute | solution.py:15
  55.8 11.1 %collective-permute-start.2 = (f32[2,16,1,256]{3,2,1,0:T(1,128)S(1)}, f32[2,16,1,256]{3,2,1,0:T(1,128)S(1)}, u32[]{:S(2)}, u32[]{:S(2)}) collective-permute-start(f32[2,16,1,256]{3,2,1,0:T(1,128)S(1)} %pad_maximum_fusion.12), channel_id=1, source_target_pairs={{0,1},{1,2},{2,3},{3,4},{4,5},{5,6},{6,7},{8,9},{9,10},{10,11},{11... | collective-permute-start | bytes 98312 | tf_op jit(solution)/shard_map/while/body/eval_jaxpr/ppermute | solution.py:15
  63.2 4.7 collective-permute-start.3
  76.0 9.9 %collective-permute-start.1 = (f32[2,16,1,256]{3,2,1,0:T(1,128)S(1)}, f32[2,16,1,256]{3,2,1,0:T(1,128)S(1)}, u32[]{:S(2)}, u32[]{:S(2)}) collective-permute-start(f32[2,16,1,256]{3,2,1,0:T(1,128)S(1)} %pad_maximum_fusion.11), channel_id=1, source_target_pairs={{1,0},{2,1},{3,2},{4,3},{5,4},{6,5},{7,6},{9,8},{10,9},{11,10},{12... | collective-permute-start | bytes 98312 | tf_op jit(solution)/shard_map/while/body/eval_jaxpr/ppermute | solution.py:15
  77.3 8.6 %collective-permute-start = (f32[2,1,16,256]{3,2,1,0:T(8,128)S(1)}, f32[2,1,16,256]{3,2,1,0:T(8,128)S(1)}, u32[]{:S(2)}, u32[]{:S(2)}) collective-permute-start(f32[2,1,16,256]{3,2,1,0:T(8,128)S(1)} %pad_maximum_fusion.10), channel_id=1, source_target_pairs={{8,0},{16,8},{24,16},{9,1},{17,9},{25,17},{10,2},{18,10},{26,18},{... | collective-permute-start | bytes 98312 | tf_op jit(solution)/shard_map/while/body/eval_jaxpr/ppermute | solution.py:15
  89.0 12.4 %collective-permute-start.2 = (f32[2,16,1,256]{3,2,1,0:T(1,128)S(1)}, f32[2,16,1,256]{3,2,1,0:T(1,128)S(1)}, u32[]{:S(2)}, u32[]{:S(2)}) collective-permute-start(f32[2,16,1,256]{3,2,1,0:T(1,128)S(1)} %pad_maximum_fusion.12), channel_id=1, source_target_pairs={{0,1},{1,2},{2,3},{3,4},{4,5},{5,6},{6,7},{8,9},{9,10},{10,11},{11... | collective-permute-start | bytes 98312 | tf_op jit(solution)/shard_map/while/body/eval_jaxpr/ppermute | solution.py:15
  96.0 6.1 %collective-permute-start.3 = (f32[2,1,16,256]{3,2,1,0:T(8,128)S(1)}, f32[2,1,16,256]{3,2,1,0:T(8,128)S(1)}, u32[]{:S(2)}, u32[]{:S(2)}) collective-permute-start(f32[2,1,16,256]{3,2,1,0:T(8,128)S(1)} %pad_maximum_fusion.13), channel_id=1, source_target_pairs={{0,8},{8,16},{16,24},{1,9},{9,17},{17,25},{2,10},{10,18},{18,26},{... | collective-permute-start | bytes 98312 | tf_op jit(solution)/shard_map/while/body/eval_jaxpr/ppermute | solution.py:15
  110.4 9.9 %collective-permute-start.1 = (f32[2,16,1,256]{3,2,1,0:T(1,128)S(1)}, f32[2,16,1,256]{3,2,1,0:T(1,128)S(1)}, u32[]{:S(2)}, u32[]{:S(2)}) collective-permute-start(f32[2,16,1,256]{3,2,1,0:T(1,128)S(1)} %pad_maximum_fusion.11), channel_id=1, source_target_pairs={{1,0},{2,1},{3,2},{4,3},{5,4},{6,5},{7,6},{9,8},{10,9},{11,10},{12... | collective-permute-start | bytes 98312 | tf_op jit(solution)/shard_map/while/body/eval_jaxpr/ppermute | solution.py:15
  111.7 8.6 %collective-permute-start = (f32[2,1,16,256]{3,2,1,0:T(8,128)S(1)}, f32[2,1,16,256]{3,2,1,0:T(8,128)S(1)}, u32[]{:S(2)}, u32[]{:S(2)}) collective-permute-start(f32[2,1,16,256]{3,2,1,0:T(8,128)S(1)} %pad_maximum_fusion.10), channel_id=1, source_target_pairs={{8,0},{16,8},{24,16},{9,1},{17,9},{25,17},{10,2},{18,10},{26,18},{... | collective-permute-start | bytes 98312 | tf_op jit(solution)/shard_map/while/body/eval_jaxpr/ppermute | solution.py:15
  123.4 12.3 %collective-permute-start.2 = (f32[2,16,1,256]{3,2,1,0:T(1,128)S(1)}, f32[2,16,1,256]{3,2,1,0:T(1,128)S(1)}, u32[]{:S(2)}, u32[]{:S(2)}) collective-permute-start(f32[2,16,1,256]{3,2,1,0:T(1,128)S(1)} %pad_maximum_fusion.12), channel_id=1, source_target_pairs={{0,1},{1,2},{2,3},{3,4},{4,5},{5,6},{6,7},{8,9},{9,10},{10,11},{11... | collective-permute-start | bytes 98312 | tf_op jit(solution)/shard_map/while/body/eval_jaxpr/ppermute | solution.py:15
  130.4 6.1 %collective-permute-start.3 = (f32[2,1,16,256]{3,2,1,0:T(8,128)S(1)}, f32[2,1,16,256]{3,2,1,0:T(8,128)S(1)}, u32[]{:S(2)}, u32[]{:S(2)}) collective-permute-start(f32[2,1,16,256]{3,2,1,0:T(8,128)S(1)} %pad_maximum_fusion.13), channel_id=1, source_target_pairs={{0,8},{8,16},{16,24},{1,9},{9,17},{17,25},{2,10},{10,18},{18,26},{... | collective-permute-start | bytes 98312 | tf_op jit(solution)/shard_map/while/body/eval_jaxpr/ppermute | solution.py:15
  144.8 9.9 %collective-permute-start.1 = (f32[2,16,1,256]{3,2,1,0:T(1,128)S(1)}, f32[2,16,1,256]{3,2,1,0:T(1,128)S(1)}, u32[]{:S(2)}, u32[]{:S(2)}) collective-permute-start(f32[2,16,1,256]{3,2,1,0:T(1,128)S(1)} %pad_maximum_fusion.11), channel_id=1, source_target_pairs={{1,0},{2,1},{3,2},{4,3},{5,4},{6,5},{7,6},{9,8},{10,9},{11,10},{12... | collective-permute-start | bytes 98312 | tf_op jit(solution)/shard_map/while/body/eval_jaxpr/ppermute | solution.py:15
  146.1 8.6 %collective-permute-start = (f32[2,1,16,256]{3,2,1,0:T(8,128)S(1)}, f32[2,1,16,256]{3,2,1,0:T(8,128)S(1)}, u32[]{:S(2)}, u32[]{:S(2)}) collective-permute-start(f32[2,1,16,256]{3,2,1,0:T(8,128)S(1)} %pad_maximum_fusion.10), channel_id=1, source_target_pairs={{8,0},{16,8},{24,16},{9,1},{17,9},{25,17},{10,2},{18,10},{26,18},{... | collective-permute-start | bytes 98312 | tf_op jit(solution)/shard_map/while/body/eval_jaxpr/ppermute | solution.py:15
  157.7 12.4 %collective-permute-start.2 = (f32[2,16,1,256]{3,2,1,0:T(1,128)S(1)}, f32[2,16,1,256]{3,2,1,0:T(1,128)S(1)}, u32[]{:S(2)}, u32[]{:S(2)}) collective-permute-start(f32[2,16,1,256]{3,2,1,0:T(1,128)S(1)} %pad_maximum_fusion.12), channel_id=1, source_target_pairs={{0,1},{1,2},{2,3},{3,4},{4,5},{5,6},{6,7},{8,9},{9,10},{10,11},{11... | collective-permute-start | bytes 98312 | tf_op jit(solution)/shard_map/while/body/eval_jaxpr/ppermute | solution.py:15
  164.8 6.1 %collective-permute-start.3 = (f32[2,1,16,256]{3,2,1,0:T(8,128)S(1)}, f32[2,1,16,256]{3,2,1,0:T(8,128)S(1)}, u32[]{:S(2)}, u32[]{:S(2)}) collective-permute-start(f32[2,1,16,256]{3,2,1,0:T(8,128)S(1)} %pad_maximum_fusion.13), channel_id=1, source_target_pairs={{0,8},{8,16},{16,24},{1,9},{9,17},{17,25},{2,10},{10,18},{18,26},{... | collective-permute-start | bytes 98312 | tf_op jit(solution)/shard_map/while/body/eval_jaxpr/ppermute | solution.py:15
  179.1 9.9 %collective-permute-start.1 = (f32[2,16,1,256]{3,2,1,0:T(1,128)S(1)}, f32[2,16,1,256]{3,2,1,0:T(1,128)S(1)}, u32[]{:S(2)}, u32[]{:S(2)}) collective-permute-start(f32[2,16,1,256]{3,2,1,0:T(1,128)S(1)} %pad_maximum_fusion.11), channel_id=1, source_target_pairs={{1,0},{2,1},{3,2},{4,3},{5,4},{6,5},{7,6},{9,8},{10,9},{11,10},{12... | collective-permute-start | bytes 98312 | tf_op jit(solution)/shard_map/while/body/eval_jaxpr/ppermute | solution.py:15
  180.5 8.6 %collective-permute-start = (f32[2,1,16,256]{3,2,1,0:T(8,128)S(1)}, f32[2,1,16,256]{3,2,1,0:T(8,128)S(1)}, u32[]{:S(2)}, u32[]{:S(2)}) collective-permute-start(f32[2,1,16,256]{3,2,1,0:T(8,128)S(1)} %pad_maximum_fusion.10), channel_id=1, source_target_pairs={{8,0},{16,8},{24,16},{9,1},{17,9},{25,17},{10,2},{18,10},{26,18},{... | collective-permute-start | bytes 98312 | tf_op jit(solution)/shard_map/while/body/eval_jaxpr/ppermute | solution.py:15
  192.1 12.3 %collective-permute-start.2 = (f32[2,16,1,256]{3,2,1,0:T(1,128)S(1)}, f32[2,16,1,256]{3,2,1,0:T(1,128)S(1)}, u32[]{:S(2)}, u32[]{:S(2)}) collective-permute-start(f32[2,16,1,256]{3,2,1,0:T(1,128)S(1)} %pad_maximum_fusion.12), channel_id=1, source_target_pairs={{0,1},{1,2},{2,3},{3,4},{4,5},{5,6},{6,7},{8,9},{9,10},{10,11},{11... | collective-permute-start | bytes 98312 | tf_op jit(solution)/shard_map/while/body/eval_jaxpr/ppermute | solution.py:15
  199.2 6.1 %collective-permute-start.3 = (f32[2,1,16,256]{3,2,1,0:T(8,128)S(1)}, f32[2,1,16,256]{3,2,1,0:T(8,128)S(1)}, u32[]{:S(2)}, u32[]{:S(2)}) collective-permute-start(f32[2,1,16,256]{3,2,1,0:T(8,128)S(1)} %pad_maximum_fusion.13), channel_id=1, source_target_pairs={{0,8},{8,16},{16,24},{1,9},{9,17},{17,25},{2,10},{10,18},{18,26},{... | collective-permute-start | bytes 98312 | tf_op jit(solution)/shard_map/while/body/eval_jaxpr/ppermute | solution.py:15
  213.5 9.9 %collective-permute-start.1 = (f32[2,16,1,256]{3,2,1,0:T(1,128)S(1)}, f32[2,16,1,256]{3,2,1,0:T(1,128)S(1)}, u32[]{:S(2)}, u32[]{:S(2)}) collective-permute-start(f32[2,16,1,256]{3,2,1,0:T(1,128)S(1)} %pad_maximum_fusion.11), channel_id=1, source_target_pairs={{1,0},{2,1},{3,2},{4,3},{5,4},{6,5},{7,6},{9,8},{10,9},{11,10},{12... | collective-permute-start | bytes 98312 | tf_op jit(solution)/shard_map/while/body/eval_jaxpr/ppermute | solution.py:15
  214.8 8.6 %collective-permute-start = (f32[2,1,16,256]{3,2,1,0:T(8,128)S(1)}, f32[2,1,16,256]{3,2,1,0:T(8,128)S(1)}, u32[]{:S(2)}, u32[]{:S(2)}) collective-permute-start(f32[2,1,16,256]{3,2,1,0:T(8,128)S(1)} %pad_maximum_fusion.10), channel_id=1, source_target_pairs={{8,0},{16,8},{24,16},{9,1},{17,9},{25,17},{10,2},{18,10},{26,18},{... | collective-permute-start | bytes 98312 | tf_op jit(solution)/shard_map/while/body/eval_jaxpr/ppermute | solution.py:15
  226.5 12.4 %collective-permute-start.2 = (f32[2,16,1,256]{3,2,1,0:T(1,128)S(1)}, f32[2,16,1,256]{3,2,1,0:T(1,128)S(1)}, u32[]{:S(2)}, u32[]{:S(2)}) collective-permute-start(f32[2,16,1,256]{3,2,1,0:T(1,128)S(1)} %pad_maximum_fusion.12), channel_id=1, source_target_pairs={{0,1},{1,2},{2,3},{3,4},{4,5},{5,6},{6,7},{8,9},{9,10},{10,11},{11... | collective-permute-start | bytes 98312 | tf_op jit(solution)/shard_map/while/body/eval_jaxpr/ppermute | solution.py:15
  233.5 6.1 %collective-permute-start.3 = (f32[2,1,16,256]{3,2,1,0:T(8,128)S(1)}, f32[2,1,16,256]{3,2,1,0:T(8,128)S(1)}, u32[]{:S(2)}, u32[]{:S(2)}) collective-permute-start(f32[2,1,16,256]{3,2,1,0:T(8,128)S(1)} %pad_maximum_fusion.13), channel_id=1, source_target_pairs={{0,8},{8,16},{16,24},{1,9},{9,17},{17,25},{2,10},{10,18},{18,26},{... | collective-permute-start | bytes 98312 | tf_op jit(solution)/shard_map/while/body/eval_jaxpr/ppermute | solution.py:15
  247.9 9.9 %collective-permute-start.1 = (f32[2,16,1,256]{3,2,1,0:T(1,128)S(1)}, f32[2,16,1,256]{3,2,1,0:T(1,128)S(1)}, u32[]{:S(2)}, u32[]{:S(2)}) collective-permute-start(f32[2,16,1,256]{3,2,1,0:T(1,128)S(1)} %pad_maximum_fusion.11), channel_id=1, source_target_pairs={{1,0},{2,1},{3,2},{4,3},{5,4},{6,5},{7,6},{9,8},{10,9},{11,10},{12... | collective-permute-start | bytes 98312 | tf_op jit(solution)/shard_map/while/body/eval_jaxpr/ppermute | solution.py:15
  249.2 8.6 %collective-permute-start = (f32[2,1,16,256]{3,2,1,0:T(8,128)S(1)}, f32[2,1,16,256]{3,2,1,0:T(8,128)S(1)}, u32[]{:S(2)}, u32[]{:S(2)}) collective-permute-start(f32[2,1,16,256]{3,2,1,0:T(8,128)S(1)} %pad_maximum_fusion.10), channel_id=1, source_target_pairs={{8,0},{16,8},{24,16},{9,1},{17,9},{25,17},{10,2},{18,10},{26,18},{... | collective-permute-start | bytes 98312 | tf_op jit(solution)/shard_map/while/body/eval_jaxpr/ppermute | solution.py:15
  260.8 12.3 %collective-permute-start.2 = (f32[2,16,1,256]{3,2,1,0:T(1,128)S(1)}, f32[2,16,1,256]{3,2,1,0:T(1,128)S(1)}, u32[]{:S(2)}, u32[]{:S(2)}) collective-permute-start(f32[2,16,1,256]{3,2,1,0:T(1,128)S(1)} %pad_maximum_fusion.12), channel_id=1, source_target_pairs={{0,1},{1,2},{2,3},{3,4},{4,5},{5,6},{6,7},{8,9},{9,10},{10,11},{11... | collective-permute-start | bytes 98312 | tf_op jit(solution)/shard_map/while/body/eval_jaxpr/ppermute | solution.py:15
  267.9 6.1 %collective-permute-start.3 = (f32[2,1,16,256]{3,2,1,0:T(8,128)S(1)}, f32[2,1,16,256]{3,2,1,0:T(8,128)S(1)}, u32[]{:S(2)}, u32[]{:S(2)}) collective-permute-start(f32[2,1,16,256]{3,2,1,0:T(8,128)S(1)} %pad_maximum_fusion.13), channel_id=1, source_target_pairs={{0,8},{8,16},{16,24},{1,9},{9,17},{17,25},{2,10},{10,18},{18,26},{... | collective-permute-start | bytes 98312 | tf_op jit(solution)/shard_map/while/body/eval_jaxpr/ppermute | solution.py:15
  282.2 9.9 %collective-permute-start.1 = (f32[2,16,1,256]{3,2,1,0:T(1,128)S(1)}, f32[2,16,1,256]{3,2,1,0:T(1,128)S(1)}, u32[]{:S(2)}, u32[]{:S(2)}) collective-permute-start(f32[2,16,1,256]{3,2,1,0:T(1,128)S(1)} %pad_maximum_fusion.11), channel_id=1, source_target_pairs={{1,0},{2,1},{3,2},{4,3},{5,4},{6,5},{7,6},{9,8},{10,9},{11,10},{12... | collective-permute-start | bytes 98312 | tf_op jit(solution)/shard_map/while/body/eval_jaxpr/ppermute | solution.py:15
  283.6 8.6 %collective-permute-start = (f32[2,1,16,256]{3,2,1,0:T(8,128)S(1)}, f32[2,1,16,256]{3,2,1,0:T(8,128)S(1)}, u32[]{:S(2)}, u32[]{:S(2)}) collective-permute-start(f32[2,1,16,256]{3,2,1,0:T(8,128)S(1)} %pad_maximum_fusion.10), channel_id=1, source_target_pairs={{8,0},{16,8},{24,16},{9,1},{17,9},{25,17},{10,2},{18,10},{26,18},{... | collective-permute-start | bytes 98312 | tf_op jit(solution)/shard_map/while/body/eval_jaxpr/ppermute | solution.py:15
  295.2 12.4 %collective-permute-start.2 = (f32[2,16,1,256]{3,2,1,0:T(1,128)S(1)}, f32[2,16,1,256]{3,2,1,0:T(1,128)S(1)}, u32[]{:S(2)}, u32[]{:S(2)}) collective-permute-start(f32[2,16,1,256]{3,2,1,0:T(1,128)S(1)} %pad_maximum_fusion.12), channel_id=1, source_target_pairs={{0,1},{1,2},{2,3},{3,4},{4,5},{5,6},{6,7},{8,9},{9,10},{10,11},{11... | collective-permute-start | bytes 98312 | tf_op jit(solution)/shard_map/while/body/eval_jaxpr/ppermute | solution.py:15
  302.3 6.1 %collective-permute-start.3 = (f32[2,1,16,256]{3,2,1,0:T(8,128)S(1)}, f32[2,1,16,256]{3,2,1,0:T(8,128)S(1)}, u32[]{:S(2)}, u32[]{:S(2)}) collective-permute-start(f32[2,1,16,256]{3,2,1,0:T(8,128)S(1)} %pad_maximum_fusion.13), channel_id=1, source_target_pairs={{0,8},{8,16},{16,24},{1,9},{9,17},{17,25},{2,10},{10,18},{18,26},{... | collective-permute-start | bytes 98312 | tf_op jit(solution)/shard_map/while/body/eval_jaxpr/ppermute | solution.py:15
  316.6 9.9 %collective-permute-start.1 = (f32[2,16,1,256]{3,2,1,0:T(1,128)S(1)}, f32[2,16,1,256]{3,2,1,0:T(1,128)S(1)}, u32[]{:S(2)}, u32[]{:S(2)}) collective-permute-start(f32[2,16,1,256]{3,2,1,0:T(1,128)S(1)} %pad_maximum_fusion.11), channel_id=1, source_target_pairs={{1,0},{2,1},{3,2},{4,3},{5,4},{6,5},{7,6},{9,8},{10,9},{11,10},{12... | collective-permute-start | bytes 98312 | tf_op jit(solution)/shard_map/while/body/eval_jaxpr/ppermute | solution.py:15
  317.9 8.6 %collective-permute-start = (f32[2,1,16,256]{3,2,1,0:T(8,128)S(1)}, f32[2,1,16,256]{3,2,1,0:T(8,128)S(1)}, u32[]{:S(2)}, u32[]{:S(2)}) collective-permute-start(f32[2,1,16,256]{3,2,1,0:T(8,128)S(1)} %pad_maximum_fusion.10), channel_id=1, source_target_pairs={{8,0},{16,8},{24,16},{9,1},{17,9},{25,17},{10,2},{18,10},{26,18},{... | collective-permute-start | bytes 98312 | tf_op jit(solution)/shard_map/while/body/eval_jaxpr/ppermute | solution.py:15
  329.6 12.3 %collective-permute-start.2 = (f32[2,16,1,256]{3,2,1,0:T(1,128)S(1)}, f32[2,16,1,256]{3,2,1,0:T(1,128)S(1)}, u32[]{:S(2)}, u32[]{:S(2)}) collective-permute-start(f32[2,16,1,256]{3,2,1,0:T(1,128)S(1)} %pad_maximum_fusion.12), channel_id=1, source_target_pairs={{0,1},{1,2},{2,3},{3,4},{4,5},{5,6},{6,7},{8,9},{9,10},{10,11},{11... | collective-permute-start | bytes 98312 | tf_op jit(solution)/shard_map/while/body/eval_jaxpr/ppermute | solution.py:15
  336.6 6.1 %collective-permute-start.3 = (f32[2,1,16,256]{3,2,1,0:T(8,128)S(1)}, f32[2,1,16,256]{3,2,1,0:T(8,128)S(1)}, u32[]{:S(2)}, u32[]{:S(2)}) collective-permute-start(f32[2,1,16,256]{3,2,1,0:T(8,128)S(1)} %pad_maximum_fusion.13), channel_id=1, source_target_pairs={{0,8},{8,16},{16,24},{1,9},{9,17},{17,25},{2,10},{10,18},{18,26},{... | collective-permute-start | bytes 98312 | tf_op jit(solution)/shard_map/while/body/eval_jaxpr/ppermute | solution.py:15
  351.0 9.9 %collective-permute-start.1 = (f32[2,16,1,256]{3,2,1,0:T(1,128)S(1)}, f32[2,16,1,256]{3,2,1,0:T(1,128)S(1)}, u32[]{:S(2)}, u32[]{:S(2)}) collective-permute-start(f32[2,16,1,256]{3,2,1,0:T(1,128)S(1)} %pad_maximum_fusion.11), channel_id=1, source_target_pairs={{1,0},{2,1},{3,2},{4,3},{5,4},{6,5},{7,6},{9,8},{10,9},{11,10},{12... | collective-permute-start | bytes 98312 | tf_op jit(solution)/shard_map/while/body/eval_jaxpr/ppermute | solution.py:15
  352.3 8.6 %collective-permute-start = (f32[2,1,16,256]{3,2,1,0:T(8,128)S(1)}, f32[2,1,16,256]{3,2,1,0:T(8,128)S(1)}, u32[]{:S(2)}, u32[]{:S(2)}) collective-permute-start(f32[2,1,16,256]{3,2,1,0:T(8,128)S(1)} %pad_maximum_fusion.10), channel_id=1, source_target_pairs={{8,0},{16,8},{24,16},{9,1},{17,9},{25,17},{10,2},{18,10},{26,18},{... | collective-permute-start | bytes 98312 | tf_op jit(solution)/shard_map/while/body/eval_jaxpr/ppermute | solution.py:15
  364.0 12.4 %collective-permute-start.2 = (f32[2,16,1,256]{3,2,1,0:T(1,128)S(1)}, f32[2,16,1,256]{3,2,1,0:T(1,128)S(1)}, u32[]{:S(2)}, u32[]{:S(2)}) collective-permute-start(f32[2,16,1,256]{3,2,1,0:T(1,128)S(1)} %pad_maximum_fusion.12), channel_id=1, source_target_pairs={{0,1},{1,2},{2,3},{3,4},{4,5},{5,6},{6,7},{8,9},{9,10},{10,11},{11... | collective-permute-start | bytes 98312 | tf_op jit(solution)/shard_map/while/body/eval_jaxpr/ppermute | solution.py:15
  371.0 6.1 %collective-permute-start.3 = (f32[2,1,16,256]{3,2,1,0:T(8,128)S(1)}, f32[2,1,16,256]{3,2,1,0:T(8,128)S(1)}, u32[]{:S(2)}, u32[]{:S(2)}) collective-permute-start(f32[2,1,16,256]{3,2,1,0:T(8,128)S(1)} %pad_maximum_fusion.13), channel_id=1, source_target_pairs={{0,8},{8,16},{16,24},{1,9},{9,17},{17,25},{2,10},{10,18},{18,26},{... | collective-permute-start | bytes 98312 | tf_op jit(solution)/shard_map/while/body/eval_jaxpr/ppermute | solution.py:15
  385.4 9.9 %collective-permute-start.1 = (f32[2,16,1,256]{3,2,1,0:T(1,128)S(1)}, f32[2,16,1,256]{3,2,1,0:T(1,128)S(1)}, u32[]{:S(2)}, u32[]{:S(2)}) collective-permute-start(f32[2,16,1,256]{3,2,1,0:T(1,128)S(1)} %pad_maximum_fusion.11), channel_id=1, source_target_pairs={{1,0},{2,1},{3,2},{4,3},{5,4},{6,5},{7,6},{9,8},{10,9},{11,10},{12... | collective-permute-start | bytes 98312 | tf_op jit(solution)/shard_map/while/body/eval_jaxpr/ppermute | solution.py:15
  386.7 8.6 %collective-permute-start = (f32[2,1,16,256]{3,2,1,0:T(8,128)S(1)}, f32[2,1,16,256]{3,2,1,0:T(8,128)S(1)}, u32[]{:S(2)}, u32[]{:S(2)}) collective-permute-start(f32[2,1,16,256]{3,2,1,0:T(8,128)S(1)} %pad_maximum_fusion.10), channel_id=1, source_target_pairs={{8,0},{16,8},{24,16},{9,1},{17,9},{25,17},{10,2},{18,10},{26,18},{... | collective-permute-start | bytes 98312 | tf_op jit(solution)/shard_map/while/body/eval_jaxpr/ppermute | solution.py:15
  398.3 12.3 %collective-permute-start.2 = (f32[2,16,1,256]{3,2,1,0:T(1,128)S(1)}, f32[2,16,1,256]{3,2,1,0:T(1,128)S(1)}, u32[]{:S(2)}, u32[]{:S(2)}) collective-permute-start(f32[2,16,1,256]{3,2,1,0:T(1,128)S(1)} %pad_maximum_fusion.12), channel_id=1, source_target_pairs={{0,1},{1,2},{2,3},{3,4},{4,5},{5,6},{6,7},{8,9},{9,10},{10,11},{11... | collective-permute-start | bytes 98312 | tf_op jit(solution)/shard_map/while/body/eval_jaxpr/ppermute | solution.py:15
  405.4 6.1 %collective-permute-start.3 = (f32[2,1,16,256]{3,2,1,0:T(8,128)S(1)}, f32[2,1,16,256]{3,2,1,0:T(8,128)S(1)}, u32[]{:S(2)}, u32[]{:S(2)}) collective-permute-start(f32[2,1,16,256]{3,2,1,0:T(8,128)S(1)} %pad_maximum_fusion.13), channel_id=1, source_target_pairs={{0,8},{8,16},{16,24},{1,9},{9,17},{17,25},{2,10},{10,18},{18,26},{... | collective-permute-start | bytes 98312 | tf_op jit(solution)/shard_map/while/body/eval_jaxpr/ppermute | solution.py:15
  419.7 9.9 %collective-permute-start.1 = (f32[2,16,1,256]{3,2,1,0:T(1,128)S(1)}, f32[2,16,1,256]{3,2,1,0:T(1,128)S(1)}, u32[]{:S(2)}, u32[]{:S(2)}) collective-permute-start(f32[2,16,1,256]{3,2,1,0:T(1,128)S(1)} %pad_maximum_fusion.11), channel_id=1, source_target_pairs={{1,0},{2,1},{3,2},{4,3},{5,4},{6,5},{7,6},{9,8},{10,9},{11,10},{12... | collective-permute-start | bytes 98312 | tf_op jit(solution)/shard_map/while/body/eval_jaxpr/ppermute | solution.py:15
  421.1 8.6 %collective-permute-start = (f32[2,1,16,256]{3,2,1,0:T(8,128)S(1)}, f32[2,1,16,256]{3,2,1,0:T(8,128)S(1)}, u32[]{:S(2)}, u32[]{:S(2)}) collective-permute-start(f32[2,1,16,256]{3,2,1,0:T(8,128)S(1)} %pad_maximum_fusion.10), channel_id=1, source_target_pairs={{8,0},{16,8},{24,16},{9,1},{17,9},{25,17},{10,2},{18,10},{26,18},{... | collective-permute-start | bytes 98312 | tf_op jit(solution)/shard_map/while/body/eval_jaxpr/ppermute | solution.py:15
  432.7 12.4 %collective-permute-start.2 = (f32[2,16,1,256]{3,2,1,0:T(1,128)S(1)}, f32[2,16,1,256]{3,2,1,0:T(1,128)S(1)}, u32[]{:S(2)}, u32[]{:S(2)}) collective-permute-start(f32[2,16,1,256]{3,2,1,0:T(1,128)S(1)} %pad_maximum_fusion.12), channel_id=1, source_target_pairs={{0,1},{1,2},{2,3},{3,4},{4,5},{5,6},{6,7},{8,9},{9,10},{10,11},{11... | collective-permute-start | bytes 98312 | tf_op jit(solution)/shard_map/while/body/eval_jaxpr/ppermute | solution.py:15
  439.7 6.1 %collective-permute-start.3 = (f32[2,1,16,256]{3,2,1,0:T(8,128)S(1)}, f32[2,1,16,256]{3,2,1,0:T(8,128)S(1)}, u32[]{:S(2)}, u32[]{:S(2)}) collective-permute-start(f32[2,1,16,256]{3,2,1,0:T(8,128)S(1)} %pad_maximum_fusion.13), channel_id=1, source_target_pairs={{0,8},{8,16},{16,24},{1,9},{9,17},{17,25},{2,10},{10,18},{18,26},{... | collective-permute-start | bytes 98312 | tf_op jit(solution)/shard_map/while/body/eval_jaxpr/ppermute | solution.py:15
  454.1 9.9 %collective-permute-start.1 = (f32[2,16,1,256]{3,2,1,0:T(1,128)S(1)}, f32[2,16,1,256]{3,2,1,0:T(1,128)S(1)}, u32[]{:S(2)}, u32[]{:S(2)}) collective-permute-start(f32[2,16,1,256]{3,2,1,0:T(1,128)S(1)} %pad_maximum_fusion.11), channel_id=1, source_target_pairs={{1,0},{2,1},{3,2},{4,3},{5,4},{6,5},{7,6},{9,8},{10,9},{11,10},{12... | collective-permute-start | bytes 98312 | tf_op jit(solution)/shard_map/while/body/eval_jaxpr/ppermute | solution.py:15
  455.4 8.6 %collective-permute-start = (f32[2,1,16,256]{3,2,1,0:T(8,128)S(1)}, f32[2,1,16,256]{3,2,1,0:T(8,128)S(1)}, u32[]{:S(2)}, u32[]{:S(2)}) collective-permute-start(f32[2,1,16,256]{3,2,1,0:T(8,128)S(1)} %pad_maximum_fusion.10), channel_id=1, source_target_pairs={{8,0},{16,8},{24,16},{9,1},{17,9},{25,17},{10,2},{18,10},{26,18},{... | collective-permute-start | bytes 98312 | tf_op jit(solution)/shard_map/while/body/eval_jaxpr/ppermute | solution.py:15
  467.1 12.3 %collective-permute-start.2 = (f32[2,16,1,256]{3,2,1,0:T(1,128)S(1)}, f32[2,16,1,256]{3,2,1,0:T(1,128)S(1)}, u32[]{:S(2)}, u32[]{:S(2)}) collective-permute-start(f32[2,16,1,256]{3,2,1,0:T(1,128)S(1)} %pad_maximum_fusion.12), channel_id=1, source_target_pairs={{0,1},{1,2},{2,3},{3,4},{4,5},{5,6},{6,7},{8,9},{9,10},{10,11},{11... | collective-permute-start | bytes 98312 | tf_op jit(solution)/shard_map/while/body/eval_jaxpr/ppermute | solution.py:15
  474.1 6.1 %collective-permute-start.3 = (f32[2,1,16,256]{3,2,1,0:T(8,128)S(1)}, f32[2,1,16,256]{3,2,1,0:T(8,128)S(1)}, u32[]{:S(2)}, u32[]{:S(2)}) collective-permute-start(f32[2,1,16,256]{3,2,1,0:T(8,128)S(1)} %pad_maximum_fusion.13), channel_id=1, source_target_pairs={{0,8},{8,16},{16,24},{1,9},{9,17},{17,25},{2,10},{10,18},{18,26},{... | collective-permute-start | bytes 98312 | tf_op jit(solution)/shard_map/while/body/eval_jaxpr/ppermute | solution.py:15
  488.5 9.9 %collective-permute-start.1 = (f32[2,16,1,256]{3,2,1,0:T(1,128)S(1)}, f32[2,16,1,256]{3,2,1,0:T(1,128)S(1)}, u32[]{:S(2)}, u32[]{:S(2)}) collective-permute-start(f32[2,16,1,256]{3,2,1,0:T(1,128)S(1)} %pad_maximum_fusion.11), channel_id=1, source_target_pairs={{1,0},{2,1},{3,2},{4,3},{5,4},{6,5},{7,6},{9,8},{10,9},{11,10},{12... | collective-permute-start | bytes 98312 | tf_op jit(solution)/shard_map/while/body/eval_jaxpr/ppermute | solution.py:15
  489.8 8.6 %collective-permute-start = (f32[2,1,16,256]{3,2,1,0:T(8,128)S(1)}, f32[2,1,16,256]{3,2,1,0:T(8,128)S(1)}, u32[]{:S(2)}, u32[]{:S(2)}) collective-permute-start(f32[2,1,16,256]{3,2,1,0:T(8,128)S(1)} %pad_maximum_fusion.10), channel_id=1, source_target_pairs={{8,0},{16,8},{24,16},{9,1},{17,9},{25,17},{10,2},{18,10},{26,18},{... | collective-permute-start | bytes 98312 | tf_op jit(solution)/shard_map/while/body/eval_jaxpr/ppermute | solution.py:15
  501.4 12.4 %collective-permute-start.2 = (f32[2,16,1,256]{3,2,1,0:T(1,128)S(1)}, f32[2,16,1,256]{3,2,1,0:T(1,128)S(1)}, u32[]{:S(2)}, u32[]{:S(2)}) collective-permute-start(f32[2,16,1,256]{3,2,1,0:T(1,128)S(1)} %pad_maximum_fusion.12), channel_id=1, source_target_pairs={{0,1},{1,2},{2,3},{3,4},{4,5},{5,6},{6,7},{8,9},{9,10},{10,11},{11... | collective-permute-start | bytes 98312 | tf_op jit(solution)/shard_map/while/body/eval_jaxpr/ppermute | solution.py:15
  508.5 6.1 %collective-permute-start.3 = (f32[2,1,16,256]{3,2,1,0:T(8,128)S(1)}, f32[2,1,16,256]{3,2,1,0:T(8,128)S(1)}, u32[]{:S(2)}, u32[]{:S(2)}) collective-permute-start(f32[2,1,16,256]{3,2,1,0:T(8,128)S(1)} %pad_maximum_fusion.13), channel_id=1, source_target_pairs={{0,8},{8,16},{16,24},{1,9},{9,17},{17,25},{2,10},{10,18},{18,26},{... | collective-permute-start | bytes 98312 | tf_op jit(solution)/shard_map/while/body/eval_jaxpr/ppermute | solution.py:15
  522.8 9.9 %collective-permute-start.1 = (f32[2,16,1,256]{3,2,1,0:T(1,128)S(1)}, f32[2,16,1,256]{3,2,1,0:T(1,128)S(1)}, u32[]{:S(2)}, u32[]{:S(2)}) collective-permute-start(f32[2,16,1,256]{3,2,1,0:T(1,128)S(1)} %pad_maximum_fusion.11), channel_id=1, source_target_pairs={{1,0},{2,1},{3,2},{4,3},{5,4},{6,5},{7,6},{9,8},{10,9},{11,10},{12... | collective-permute-start | bytes 98312 | tf_op jit(solution)/shard_map/while/body/eval_jaxpr/ppermute | solution.py:15
  524.2 8.6 %collective-permute-start = (f32[2,1,16,256]{3,2,1,0:T(8,128)S(1)}, f32[2,1,16,256]{3,2,1,0:T(8,128)S(1)}, u32[]{:S(2)}, u32[]{:S(2)}) collective-permute-start(f32[2,1,16,256]{3,2,1,0:T(8,128)S(1)} %pad_maximum_fusion.10), channel_id=1, source_target_pairs={{8,0},{16,8},{24,16},{9,1},{17,9},{25,17},{10,2},{18,10},{26,18},{... | collective-permute-start | bytes 98312 | tf_op jit(solution)/shard_map/while/body/eval_jaxpr/ppermute | solution.py:15
  535.8 12.3 %collective-permute-start.2 = (f32[2,16,1,256]{3,2,1,0:T(1,128)S(1)}, f32[2,16,1,256]{3,2,1,0:T(1,128)S(1)}, u32[]{:S(2)}, u32[]{:S(2)}) collective-permute-start(f32[2,16,1,256]{3,2,1,0:T(1,128)S(1)} %pad_maximum_fusion.12), channel_id=1, source_target_pairs={{0,1},{1,2},{2,3},{3,4},{4,5},{5,6},{6,7},{8,9},{9,10},{10,11},{11... | collective-permute-start | bytes 98312 | tf_op jit(solution)/shard_map/while/body/eval_jaxpr/ppermute | solution.py:15
  542.9 6.1 %collective-permute-start.3 = (f32[2,1,16,256]{3,2,1,0:T(8,128)S(1)}, f32[2,1,16,256]{3,2,1,0:T(8,128)S(1)}, u32[]{:S(2)}, u32[]{:S(2)}) collective-permute-start(f32[2,1,16,256]{3,2,1,0:T(8,128)S(1)} %pad_maximum_fusion.13), channel_id=1, source_target_pairs={{0,8},{8,16},{16,24},{1,9},{9,17},{17,25},{2,10},{10,18},{18,26},{... | collective-permute-start | bytes 98312 | tf_op jit(solution)/shard_map/while/body/eval_jaxpr/ppermute | solution.py:15
  (424 other events, 2371.5 us)
